TPU v7x, 16 devices: a whole 2x2x2 slice. The times are simulated.
16 devices in a mesh: batch: 4 (over z, y), seq: 4 (over x, core).
Axes of the slice: x: 2, y: 2, z: 2, core: 2. Of those that a mesh axis runs over, the one named last changes fastest.
Arguments:
- hidden: bfloat16 [128, 2048], P('batch'), parts along dimension 0
- lengths: int32 [128], P('batch'), parts along dimension 0
- c_kv: bfloat16 [128, 4096, 512], P('batch', 'seq'), parts along dimension 0
- k_rope: bfloat16 [128, 4096, 64], P('batch', 'seq'), parts along dimension 0
- w_uq: bfloat16 [2048, 16, 128], P(None, 'seq')
- w_qr: bfloat16 [2048, 16, 64], P(None, 'seq')
- w_uk: bfloat16 [16, 128, 512], P('seq')
- w_uv: bfloat16 [16, 512, 128], P('seq')
- w_o: bfloat16 [16, 128, 2048], P('seq')
Outputs:
- output: bfloat16 [128, 2048], P('batch'), parts along dimension 0
There are 4 independent parts. A program takes and returns all parts, laid end to end along the dimension named above; an argument that names none is the same for every part.
All inputs are finite; a program needn't handle non-finite values.
Results may differ from a plain program's by a relative error of at most 0.00323331.
Values are sent between devices in bfloat16 or wider.
A program may use at most 1 GiB of HBM per device.

v0:
```python
import math
import jax
import jax.numpy as jnp
from jax import lax
from jax.sharding import PartitionSpec as P


def solution(mesh):
    row_spec = P('batch', None)
    cache_spec = P('batch', 'seq', None)
    in_specs = (row_spec, P('batch'), cache_spec, cache_spec, P(None, 'seq', None), P(None, 'seq', None), P('seq', None, None), P('seq', None, None), P('seq', None, None))

    def mla_step(hidden, lengths, c_kv, k_rope, w_uq, w_qr, w_uk, w_uv, w_o):
        shard_len = c_kv.shape[1]
        lat_dim = c_kv.shape[2]
        score_scale = 1.0 / math.sqrt(w_uq.shape[2] + w_qr.shape[2])
        q_nope = jnp.einsum('bd,dhk->bhk', hidden, w_uq, preferred_element_type=jnp.float32).astype(jnp.bfloat16)
        q_rope = jnp.einsum('bd,dhr->bhr', hidden, w_qr, preferred_element_type=jnp.float32).astype(jnp.bfloat16)
        q_lat = jnp.einsum('bhk,hkc->bhc', q_nope, w_uk, preferred_element_type=jnp.float32).astype(jnp.bfloat16)
        q_local = jnp.concatenate([q_lat, q_rope], axis=2)
        q_all = lax.all_gather(q_local, 'seq', axis=1, tiled=True)
        scores = (jnp.einsum('bhc,btc->bht', q_all[:, :, :lat_dim], c_kv, preferred_element_type=jnp.float32) + jnp.einsum('bhr,btr->bht', q_all[:, :, lat_dim:], k_rope, preferred_element_type=jnp.float32)) * score_scale
        positions = lax.axis_index('seq') * shard_len + jnp.arange(shard_len)
        is_valid = positions[None, None, :] < lengths[:, None, None]
        scores = jnp.where(is_valid, scores, -jnp.inf)
        local_max = jnp.max(scores, axis=2)
        exp_shift = jnp.where(local_max > -jnp.inf, local_max, 0.0)
        p_weights = jnp.exp(scores - exp_shift[:, :, None])
        weight_sum = jnp.sum(p_weights, axis=2)
        latent_sum = jnp.einsum('bht,btc->bhc', p_weights.astype(jnp.bfloat16), c_kv, preferred_element_type=jnp.float32)
        global_max = lax.pmax(local_max, 'seq')
        rescale = jnp.exp(local_max - global_max)
        packed = jnp.concatenate([latent_sum * rescale[:, :, None], (weight_sum * rescale)[:, :, None]], axis=2)
        merged = lax.psum_scatter(packed, 'seq', scatter_dimension=1, tiled=True)
        o_lat = (merged[:, :, :lat_dim] / merged[:, :, lat_dim:]).astype(jnp.bfloat16)
        o_val = jnp.einsum('bhc,hcv->bhv', o_lat, w_uv, preferred_element_type=jnp.float32).astype(jnp.bfloat16)
        y_part = jnp.einsum('bhv,hvd->bd', o_val, w_o, preferred_element_type=jnp.float32)
        y_sum = lax.psum(y_part, 'seq')
        return (hidden.astype(jnp.float32) + y_sum).astype(jnp.bfloat16)

    return jax.shard_map(mla_step, mesh=mesh, in_specs=in_specs, out_specs=row_spec, check_vma=False)
```

profile of v0, /device:TPU:0, one launch (start us, length us, event | category | flops | bytes accessed | tf_op | source)
XLA Modules:
  0.0 133.1 jit_solution(8698831234432996894)
XLA Ops:
  6.5 0.0 copy-start
  6.5 0.0 reduce-scatter.2.cloned.1.call-start
  6.5 2.0 %convolution_convert_fusion.2 = bf16[32,4,64]{2,0,1:T(8,128)(2,1)S(1)} fusion(bf16[2048,4,64]{0,2,1:T(8,128)(2,1)} %param.14, bf16[32,2048]{1,0:T(8,128)(2,1)} %param.9), kind=kOutput, calls=%fused_computation.13 | convolution fusion | flops 33562624 | bytes 1196032 | tf_op jit(solution)/shard_map/bd,dhr->bhr/dot_general | solution.py:18
  8.6 0.0 copy-done
  8.6 0.0 copy-start.4
  8.6 1.8 %fusion.4 = bf16[32,4,512]{2,0,1:T(8,128)(2,1)S(1)} fusion(bf16[4,128,512]{2,1,0:T(8,128)(2,1)} %param.15, bf16[2048,4,128]{2,1,0:T(4,128)(2,1)S(1)} %copy-done, bf16[32,2048]{1,0:T(8,128)(2,1)} %param.9), kind=kOutput, calls=%fused_computation.10 | convolution fusion | flops 83968000 | bytes 2883584 | tf_op jit(solution)/shard_map/bhk,hkc->bhc/dot_general | solution.py:19
  10.4 9.6 %all_gather.3 = bf16[32,16,576]{2,0,1:T(8,128)(2,1)S(1)} all-gather(bf16[32,4,576]{2,0,1:T(8,128)(2,1)S(1)} %pad_maximum_fusion.1), channel_id=1, replica_groups=mesh['batch'=4,'seq'=4] {'seq'}, dimensions={1}, use_global_device_ids=true | all-gather | bytes 737280 | tf_op jit(solution)/shard_map/all_gather | solution.py:21
  20.1 0.0 copy-done.4
  20.1 0.1 broadcast_compare_fusion
  20.2 15.5 %fusion.13 = f32[32,16,1024]{2,1,0:T(8,128)} fusion(bf16[32,1024,512]{2,1,0:T(8,128)(2,1)} %param.11, bf16[32,16,512]{2,0,1:T(8,128)(2,1)S(1)} %slice.16), kind=kOutput, calls=%fused_computation.16 | convolution fusion | flops 536870912 | bytes 36175872 | tf_op jit(solution)/shard_map/bhc,btc->bht/dot_general | solution.py:22
  35.7 5.0 %fusion.24 = (f32[32,16]{1,0:T(8,128)S(1)}, f32[32,16,1024]{2,1,0:T(8,128)}) fusion(f32[32,16,1024]{2,1,0:T(8,128)} %fusion.13, bf16[32,1024,64]{1,2,0:T(8,128)(2,1)} %param.12, bf16[32,16,64]{2,0,1:T(8,128)(2,1)S(1)} %slice.17, pred[32,1024]{1,0:T(8,128)(4,1)S(1)} %broadcast_compare_fusion), kind=kOutput, calls=%fused_computation.32 | convolution fusion | flops 69205504 | bytes 8488960 | tf_op jit(solution)/shard_map/bhr,btr->bht/dot_general | solution.py:22
  40.7 11.0 %pmax.7 = f32[32,16]{1,0:T(8,128)S(1)} all-reduce(f32[32,16]{1,0:T(8,128)S(1)} %get-tuple-element.7), channel_id=1, replica_groups=mesh['batch'=4,'seq'=4] {'seq'}, use_global_device_ids=true, to_apply=%region_1.2 | all-reduce | flops 512 | bytes 4096 | tf_op jit(solution)/shard_map/pmax | solution.py:31
  51.7 0.0 copy-start.1
  51.7 2.2 %fusion.2 = f32[32,16]{1,0:T(8,128)S(1)} fusion(f32[32,16,1024]{2,1,0:T(8,128)} %get-tuple-element.8, f32[32,16]{1,0:T(8,128)S(1)} %compare_select_fusion), kind=kLoop, calls=%fused_computation.5 | loop fusion | flops 1048064 | bytes 2101248 | tf_op jit(solution)/shard_map/reduce_sum | solution.py:29
  53.9 0.0 copy-done.1
  54.0 12.8 %convolution_multiply_fusion = f32[32,16,512]{2,1,0:T(8,128)S(1)} fusion(bf16[32,1024,512]{2,1,0:T(8,128)(2,1)} %param.11, f32[32,16,1024]{2,1,0:T(8,128)S(1)} %copy-done.1, f32[32,16]{1,0:T(8,128)S(1)} %compare_select_fusion, f32[32,16]{1,0:T(8,128)S(1)} %get-tuple-element.6), kind=kOutput, calls=%fused_computation.7 | convolution fusion | flops 538181632 | bytes 36704256 | tf_op jit(solution)/shard_map/bht,btc->bhc/dot_general | solution.py:30
  66.8 0.3 copy.31
  67.1 0.1 pad_maximum_fusion
  67.2 0.0 copy-start.3
  67.2 1.5 %copy.32 = f32[32,16,513]{2,0,1:T(8,128)} copy(f32[32,16,513]{2,1,0:T(8,128)S(1)} %pad_maximum_fusion) | data formatting | bytes 2101248 | tf_op jit(solution)/shard_map/concatenate | solution.py:33
  68.7 0.0 copy-start.2
  68.7 0.0 reduce-scatter.2.cloned.1.call-update
  68.7 0.0 all-reduce.2.cloned.1.call-start
  68.8 23.2 %reduce-scatter.2.cloned.1.call-done = f32[32,4,513]{2,0,1:T(8,128)} async-done(((f32[32,16,513]{2,0,1:T(8,128)}), f32[32,4,513]{2,0,1:T(8,128)}) %reduce-scatter.2.cloned.1.call-update) | async-done | bytes 262672 | tf_op jit(solution)/shard_map/reduce_scatter | solution.py:34
  92.0 0.9 slice_reduce_fusion
  92.9 0.0 copy-done.3
  92.9 3.0 %convolution_bitcast_fusion = f32[32,2048]{1,0:T(8,128)} fusion(bf16[4,128,2048]{2,1,0:T(8,128)(2,1)} %param.17, bf16[4,512,128]{2,1,0:T(8,128)(2,1)S(1)} %copy-done.3, f32[32,4,513]{2,0,1:T(8,128)} %reduce-scatter.2.cloned.1.call-done, f32[32,4]{0,1:T(4,128)S(1)} %slice_reduce_fusion), kind=kOutput, calls=%fused_computation | convolution fusion | flops 84033536 | bytes 3146240 | tf_op jit(solution)/shard_map/bhv,hvd->bd/dot_general | solution.py:37
  96.0 0.0 all-reduce.2.cloned.1.call-update
  96.0 28.6 %all-reduce.2.cloned.1.call-done = f32[32,2048]{1,0:T(8,128)} async-done(((f32[32,2048]{1,0:T(8,128)}), f32[32,2048]{1,0:T(8,128)}) %all-reduce.2.cloned.1.call-update) | async-done | bytes 262160 | tf_op jit(solution)/shard_map/psum | solution.py:38
  124.6 0.0 copy-done.2
  124.6 1.6 %add_convert_fusion = bf16[32,2048]{1,0:T(8,128)(2,1)} fusion(f32[32,2048]{1,0:T(8,128)} %all-reduce.2.cloned.1.call-done, bf16[32,2048]{1,0:T(8,128)(2,1)S(1)} %copy-done.2), kind=kLoop, calls=%fused_computation.20 | loop fusion | flops 196608 | bytes 524288 | tf_op jit(solution)/shard_map/convert_element_type | solution.py:39
  (6 shorter events, 0.1 us)
Async XLA Ops:
  6.5 2.0 %copy-start = (bf16[2048,4,128]{2,1,0:T(4,128)(2,1)S(1)}, bf16[2048,4,128]{2,1,0:T(4,128)(2,1)}, u32[]{:S(2)}) copy-start(bf16[2048,4,128]{2,1,0:T(4,128)(2,1)} %param.13) | copy-start | bytes 6291460
  6.5 85.5 %reduce-scatter.2.cloned.1.call-start = ((), (), s32[]{:S(2)}) async-start(), calls=%async_computation.1 | async-start | bytes 1638400 | tf_op jit(solution)/shard_map/reduce_scatter | solution.py:34
  8.6 11.5 %copy-start.4 = (s32[32]{0:T(128)S(1)}, s32[32]{0:T(128)}, u32[]{:S(2)}) copy-start(s32[32]{0:T(128)} %param.10) | copy-start | bytes 388
  51.7 2.2 %copy-start.1 = (f32[32,16,1024]{2,1,0:T(8,128)S(1)}, f32[32,16,1024]{2,1,0:T(8,128)}, u32[]{:S(2)}) copy-start(f32[32,16,1024]{2,1,0:T(8,128)} %get-tuple-element.8) | copy-start | bytes 6291460
  67.2 25.7 %copy-start.3 = (bf16[4,512,128]{2,1,0:T(8,128)(2,1)S(1)}, bf16[4,512,128]{2,1,0:T(8,128)(2,1)}, u32[]{:S(2)}) copy-start(bf16[4,512,128]{2,1,0:T(8,128)(2,1)} %param.16) | copy-start | bytes 1572868
  68.7 55.9 %copy-start.2 = (bf16[32,2048]{1,0:T(8,128)(2,1)S(1)}, bf16[32,2048]{1,0:T(8,128)(2,1)}, u32[]{:S(2)}) copy-start(bf16[32,2048]{1,0:T(8,128)(2,1)} %param.9) | copy-start | bytes 393220
  68.7 55.8 %all-reduce.2.cloned.1.call-start = ((), (), s32[]{:S(2)}) async-start(), calls=%async_computation.2 | async-start | bytes 524288 | tf_op jit(solution)/shard_map/psum | solution.py:38
Sparse Core Ops, SparseCore 0:
  68.9 23.0 reduce-scatter.1
  96.1 28.4 all-reduce.1
where the time goes:
time: 133 us
  waiting for transfers between devices  51.8 us (39%)
  matrix products  40.2 us (30%)
  blocking collectives  20.6 us (15%)
  between operations  13.5 us (10%)
  other arithmetic  4.06 us (3%)
  local copies, waits for them, and re-layouts  2.81 us (2%)
    psum x1, waiting for transfers between devices, mla_step(): y_sum = lax.psum(y_part, 'seq')  28.6 us
    reduce_scatter x1, waiting for transfers between devices, mla_step(): merged = lax.psum_scatter(packed, 'seq', scatter_dimension=1, tiled=True)  23.2 us
    dot_general x1, matrix products, mla_step(): jnp.einsum('bhc,btc->bht', q_all[:, :, :lat_dim], c_kv, preferred_element...  15.5 us
    dot_general x1, matrix products, mla_step(): jnp.einsum('bht,btc->bhc', p_weights.astype(jnp.bfloat16), c_kv, preferre...  12.8 us
    pmax x1, blocking collectives, mla_step(): global_max = lax.pmax(local_max, 'seq')  11 us
    all_gather x1, blocking collectives, mla_step(): q_all = lax.all_gather(q_local, 'seq', axis=1, tiled=True)  9.62 us
    dot_general x1, matrix products, mla_step(): jnp.einsum('bhr,btr->bht', q_all[:, :, lat_dim:], k_rope, preferred_eleme...  5.03 us
    dot_general x1, matrix products, mla_step(): jnp.einsum('bhv,hvd->bd', o_val, w_o, preferred_element_type=jnp.float32)  3.05 us
  transfers between devices with their start and end apart: 2, of which 2 were waited for; matrix products, arithmetic and copies ran while one was open for 0% of the time, Pallas kernels for 0%

commit v1 on v0

v1 whole, which is shorter than its diff:
```python
import math

import jax
import jax.numpy as jnp
from jax import lax
from jax.experimental import pallas as pl
from jax.experimental.pallas import tpu as pltpu
from jax.sharding import PartitionSpec as P

MESH = pl.DeviceIdType.MESH
F32 = jnp.float32
BF16 = jnp.bfloat16
GROUP = 4
STAT = 128


def dot(a, b):
    return jnp.dot(a, b, preferred_element_type=F32)


def dot_t(a, b):
    return lax.dot_general(a, b, (((1,), (1,)), ((), ())), preferred_element_type=F32)


def iota(shape, dim):
    return lax.broadcasted_iota(jnp.int32, shape, dim)


def kernel(
    len_hbm, hid_hbm, hid3_hbm, wuq_hbm, wqr_hbm, wuk_hbm, wuv_hbm, wo_hbm, ckv_hbm, kr_hbm,
    out_ref,
    len_s, hid_v, hid3_v, wuq_v, wqr_v, wuk_v, wuv_v, wo_v, ckv_v, kr_v,
    em_v, qall, sbuf, acc_src, r1, s2, keep_v, r2, y_src, yr1, yc, yr2, f_src, f_rcv,
    w_sem, ckv_sem, kr_sem, q_send, q_recv, a_send, a_recv, c_send, c_recv, y_send, y_recv,
):
    n_rows = ckv_hbm.shape[0]
    shard = ckv_hbm.shape[1]
    lat = ckv_hbm.shape[2]
    rope = kr_hbm.shape[1]
    nope = wuq_hbm.shape[1]
    n_pair = n_rows // 2
    n_group = n_pair // GROUP
    d_model = hid_hbm.shape[1]
    half_d = d_model // 2
    scale = 1.0 / math.sqrt(nope + rope)

    me = lax.axis_index("seq")
    x = lax.div(me, 2)
    c = lax.rem(me, 2)
    sib = 2 * x + (1 - c)
    cnt = 2 * (1 - x) + c

    def load(src, dst, sem):
        return pltpu.make_async_copy(src, dst, sem)

    weights = [
        load(hid_hbm, hid_v, w_sem.at[0]),
        load(wuq_hbm, wuq_v, w_sem.at[1]),
        load(wqr_hbm, wqr_v, w_sem.at[2]),
        load(wuk_hbm, wuk_v, w_sem.at[3]),
        load(len_hbm, len_s, w_sem.at[4]),
        load(hid3_hbm, hid3_v, w_sem.at[5]),
    ]
    late_weights = [
        load(wuv_hbm, wuv_v, w_sem.at[6]),
        load(wo_hbm, wo_v, w_sem.at[7]),
    ]

    def ckv_load(b):
        return load(ckv_hbm.at[b], ckv_v.at[b], ckv_sem.at[b])

    def kr_load(b):
        return load(kr_hbm.at[b], kr_v.at[b], kr_sem.at[b])

    for w in weights:
        w.start()

    barrier = pltpu.get_barrier_semaphore()
    for peer in (sib, cnt):
        pl.semaphore_signal(barrier, inc=1, device_id={"seq": peer}, device_id_type=MESH)

    def start_rows(b, carry):
        kr_load(b).start()
        ckv_load(b).start()
        return carry

    lax.fori_loop(0, n_rows // 2, start_rows, 0)
    for w in late_weights:
        w.start()
    lax.fori_loop(n_rows // 2, n_rows, start_rows, 0)

    def remote(src, dst, send, recv, peer):
        return pltpu.make_async_remote_copy(
            src_ref=src, dst_ref=dst, send_sem=send, recv_sem=recv,
            device_id={"seq": peer}, device_id_type=MESH,
        )

    n_head = wqr_hbm.shape[0] // rope
    n_local = n_rows * n_head
    lane_h = iota((n_rows, 4 * nope), 1) % n_head
    spread = (iota((nope, n_head * nope), 1) // n_head == iota((nope, n_head * nope), 0)).astype(F32).astype(BF16)
    for i in (0, 1):
        weights[i].wait()
    for k in range(d_model // nope):
        wide = dot(hid_v[:, k * nope:(k + 1) * nope], spread)
        for h in range(n_head):
            em_v[h * n_rows:(h + 1) * n_rows, k * n_head * nope:(k + 1) * n_head * nope] = jnp.where(
                lane_h == h, wide, 0.0).astype(BF16)
    q_n = dot(em_v[...], wuq_v[...]).astype(BF16)
    for i in (2, 3, 4, 5):
        weights[i].wait()
    q_r = dot_t(hid_v[...], wqr_v[...]).astype(BF16)

    def row_of(r):
        j = (r // 4) % 2
        return 2 * (r // 8) + j + x - 2 * j * x

    r_id = iota((n_local, n_local), 0)
    col = iota((n_local, n_local), 1)
    perm = (col == (r_id % 4) * n_rows + row_of(r_id)).astype(F32).astype(BF16)
    q_p = dot(perm, q_n)
    r_h = iota((n_local, nope), 0) % 4
    q_wide = jnp.concatenate([jnp.where(r_h == h, q_p, 0.0).astype(BF16) for h in range(n_head)], axis=1)
    q_l = dot(q_wide, wuk_v[...]).astype(BF16)
    r_id = iota((n_local, n_rows), 0)
    rep = (iota((n_local, n_rows), 1) == row_of(r_id)).astype(F32).astype(BF16)
    q_r = dot(rep, q_r)
    q_r = jnp.where(iota((n_local, n_head * rope), 1) // rope == iota((n_local, n_head * rope), 0) % 4, q_r, 0.0)
    fold = (iota((n_head * rope, STAT), 0) % rope == iota((n_head * rope, STAT), 1)).astype(F32).astype(BF16)
    q_r = dot(q_r.astype(BF16), fold).astype(BF16)
    for p in range(n_pair):
        qall[me, p, :, 0:lat] = q_l[8 * p:8 * p + 8]
        qall[me, p, :, lat:lat + STAT] = q_r[8 * p:8 * p + 8]

    pl.semaphore_wait(barrier, 2)

    def q_copy(kind, g):
        slot, peer = ((me, sib), (me, cnt), (cnt, sib))[kind]
        part = qall.at[slot, pl.ds(GROUP * g, GROUP)]
        return remote(part, part, q_send.at[kind, g], q_recv.at[kind, g], peer)

    for g in range(n_group):
        q_copy(1, g).start()
    for g in range(n_group):
        q_copy(0, g).start()

    upper8 = iota((8, lat + STAT), 0) < 4

    def scores(p):
        tiles = [qall[s, p].astype(F32) for s in range(4)]
        q_even = jnp.concatenate([jnp.where(upper8, tiles[0], tiles[2]), jnp.where(upper8, tiles[1], tiles[3])], axis=0)
        q_odd = jnp.concatenate([jnp.where(upper8, tiles[2], tiles[0]), jnp.where(upper8, tiles[3], tiles[1])], axis=0)
        for i, q in enumerate((q_even, q_odd)):
            q = q.astype(BF16)
            b = 2 * p + i
            s = dot_t(q[:, :lat], ckv_v[b]) + dot(q[:, lat:lat + rope], kr_v[b])
            sbuf[p % 2, i] = s

    def wait_rows(p):
        for i in (0, 1):
            kr_load(2 * p + i).wait()
            ckv_load(2 * p + i).wait()

    stat_lane = iota((16, STAT), 1) < STAT // 2

    def attend(p):
        for i in (0, 1):
            b = 2 * p + i
            s = sbuf[p % 2, i] * scale
            pos = me * shard + iota(s.shape, 1)
            s = jnp.where(pos < len_s[b], s, -jnp.inf)
            m = jnp.max(s, axis=1, keepdims=True)
            e = jnp.exp(s - jnp.where(m > -jnp.inf, m, 0.0))
            l = jnp.sum(e, axis=1, keepdims=True)
            acc = dot(e.astype(BF16), ckv_v[b])
            stat = jnp.where(stat_lane, m, l)
            for k in (0, 1):
                acc_src[k, b, :, 0:lat] = acc[8 * k:8 * k + 8]
                acc_src[k, b, :, lat:lat + STAT] = stat[8 * k:8 * k + 8]

    def pair_copy(p):
        rows = pl.ds(2 * p, 2)
        return remote(acc_src.at[1 - c, rows], r1.at[rows], a_send.at[p], a_recv.at[p], sib)

    def chip_copy(p):
        return remote(s2.at[p], r2.at[p], c_send.at[p], c_recv.at[p], cnt)

    def merge(a, b):
        m1, l1 = a[:, lat:lat + 1], a[:, lat + STAT // 2:lat + STAT // 2 + 1]
        m2, l2 = b[:, lat:lat + 1], b[:, lat + STAT // 2:lat + STAT // 2 + 1]
        m = jnp.maximum(m1, m2)
        shift = jnp.where(m > -jnp.inf, m, 0.0)
        w1, w2 = jnp.exp(m1 - shift), jnp.exp(m2 - shift)
        return w1 * a[:, :lat] + w2 * b[:, :lat], m, w1 * l1 + w2 * l2

    stat_lane8 = iota((8, STAT), 1) < STAT // 2

    def merge_pair(p):
        pair_copy(p).wait_recv()
        both = []
        for i in (0, 1):
            acc, m, l = merge(acc_src[c, 2 * p + i], r1[2 * p + i])
            both.append((acc, jnp.where(stat_lane8, m, l)))
        for k, (lo, hi) in enumerate(((0, lat), (lat, lat + STAT))):
            upper = upper8[:, lo:hi]
            zero = jnp.where(upper, both[0][k], both[1][k])
            one = jnp.where(upper, both[1][k], both[0][k])
            keep_v[p, :, lo:hi] = jnp.where(x == 0, zero, one)
            s2[p, :, lo:hi] = jnp.where(x == 0, one, zero)
        chip_copy(p).start()

    def o_rows(p):
        chip_copy(p).wait_recv()
        acc, _, l = merge(keep_v[p], r2[p])
        return acc / l

    n_out = 8 * GROUP

    def project(g):
        o_lat = jnp.concatenate([o_rows(GROUP * g + i) for i in range(GROUP)], axis=0).astype(BF16)
        head = iota((n_out, nope), 0) % 4
        wide = jnp.concatenate(
            [jnp.where(head == h, dot(o_lat, wuv_v[h]), 0.0).astype(BF16) for h in range(n_head)], axis=1)
        r = iota((8, n_out), 1)
        gather = (iota((8, n_out), 0) == row_of(r)).astype(F32).astype(BF16)
        o_val = dot(gather, wide).astype(BF16)
        for k in (0, 1):
            y_src[g, k] = dot(o_val, wo_v[:, k * half_d:(k + 1) * half_d])

    def y_copy(kind, g):
        if kind == 0:
            src, dst, peer = y_src.at[g, 1 - c], yr1.at[g], sib
        elif kind == 1:
            src, dst, peer = yc.at[g], yr2.at[g], cnt
        else:
            src, dst, peer = f_src.at[g], f_rcv.at[g], sib
        return remote(src, dst, y_send.at[kind, g], y_recv.at[kind, g], peer)

    def y_chip(g):
        y_copy(0, g).wait_recv()
        yc[g] = y_src[g, c] + yr1[g]
        y_copy(1, g).start()

    def y_final(g):
        y_copy(1, g).wait_recv()
        hid = hid3_v[c, g].astype(F32)
        f_src[g] = (hid + (yc[g] + yr2[g])).astype(BF16)
        y_copy(2, g).start()

    def store(g):
        y_copy(2, g).wait_recv()
        mine, other = f_src[g].astype(F32), f_rcv[g].astype(F32)
        out_ref[g, :, 0:half_d] = jnp.where(c == 0, mine, other).astype(BF16)
        out_ref[g, :, half_d:d_model] = jnp.where(c == 0, other, mine).astype(BF16)

    def step(j, carry, with_merge):
        wait_rows(j)
        scores(j)
        attend(j - 1)
        pair_copy(j - 1).start()
        if with_merge:
            merge_pair(j - GROUP)
        return carry

    for g in range(n_group):
        q_copy(1, g).wait_recv()
        q_copy(2, g).start()
        q_copy(0, g).wait_recv()
        q_copy(2, g).wait_recv()
        if g == 0:
            wait_rows(0)
            scores(0)
        lax.fori_loop(max(1, GROUP * g), GROUP * (g + 1), lambda j, cy, m=g > 0: step(j, cy, m), 0)
        if g == 2:
            for w in late_weights:
                w.wait()
        if g >= 2:
            project(g - 2)
            y_copy(0, g - 2).start()
        if g >= 3:
            y_chip(g - 3)
    attend(n_pair - 1)
    pair_copy(n_pair - 1).start()
    for p in range(n_pair - GROUP, n_pair - 1):
        merge_pair(p)
    for g in range(n_group - 2, n_group):
        if g == n_group - 1:
            merge_pair(n_pair - 1)
            y_chip(n_group - 3)
            y_chip(n_group - 2)
            y_final(n_group - 4)
        project(g)
        y_copy(0, g).start()
    y_final(n_group - 3)
    y_final(n_group - 2)
    y_chip(n_group - 1)
    y_final(n_group - 1)
    for g in range(n_group):
        store(g)

    for g in range(n_group):
        for kind in range(3):
            q_copy(kind, g).wait_send()
            y_copy(kind, g).wait_send()

    def drain(p, carry):
        pair_copy(p).wait_send()
        chip_copy(p).wait_send()
        return carry

    lax.fori_loop(0, n_pair, drain, 0)


def solution(mesh):
    row_spec = P('batch', None)
    cache_spec = P('batch', 'seq', None)
    in_specs = (row_spec, P('batch'), cache_spec, cache_spec, P(None, 'seq', None), P(None, 'seq', None), P('seq', None, None), P('seq', None, None), P('seq', None, None))

    def mla_step(hidden, lengths, c_kv, k_rope, w_uq, w_qr, w_uk, w_uv, w_o):
        n_rows, d_model = hidden.shape
        _, shard, lat = c_kv.shape
        rope = k_rope.shape[2]
        n_head, nope = w_uq.shape[1], w_uq.shape[2]
        n_pair = n_rows // 2
        n_group = n_pair // GROUP
        wide = lat + STAT
        half = d_model // 2
        hid3 = jnp.transpose(hidden.reshape(n_group, 8, 2, half), (2, 0, 1, 3))
        operands = (
            lengths,
            hidden,
            hid3,
            w_uq.reshape(d_model * n_head, nope),
            jnp.transpose(w_qr, (1, 2, 0)).reshape(n_head * rope, d_model),
            w_uk.reshape(n_head * nope, lat),
            w_uv,
            w_o.reshape(n_head * w_o.shape[1], d_model),
            c_kv,
            jnp.transpose(k_rope, (0, 2, 1)),
        )
        vm = pltpu.VMEM
        dma = pltpu.SemaphoreType.DMA
        out = pl.pallas_call(
            kernel,
            out_shape=jax.ShapeDtypeStruct((n_group, 8, d_model), BF16),
            in_specs=[pl.BlockSpec(memory_space=pltpu.HBM)] * len(operands),
            out_specs=pl.BlockSpec(memory_space=pltpu.VMEM),
            scratch_shapes=[
                pltpu.SMEM((n_rows,), jnp.int32),
                vm(hidden.shape, BF16),
                vm(hid3.shape, BF16),
                vm(operands[3].shape, BF16),
                vm(operands[4].shape, BF16),
                vm(operands[5].shape, BF16),
                vm(operands[6].shape, BF16),
                vm(operands[7].shape, BF16),
                vm(c_kv.shape, BF16),
                vm(operands[9].shape, BF16),
                vm((n_head * n_rows, n_head * d_model), BF16),
                vm((4, n_pair, 8, wide), BF16),
                vm((2, 2, 16, shard), F32),
                vm((2, n_rows, 8, wide), F32),
                vm((n_rows, 8, wide), F32),
                vm((n_pair, 8, wide), F32),
                vm((n_pair, 8, wide), F32),
                vm((n_pair, 8, wide), F32),
                vm((n_group, 2, 8, half), F32),
                vm((n_group, 8, half), F32),
                vm((n_group, 8, half), F32),
                vm((n_group, 8, half), F32),
                vm((n_group, 8, half), BF16),
                vm((n_group, 8, half), BF16),
                dma((8,)),
                dma((n_rows,)),
                dma((n_rows,)),
                dma((3, n_group)),
                dma((3, n_group)),
                dma((n_pair,)),
                dma((n_pair,)),
                dma((n_pair,)),
                dma((n_pair,)),
                dma((3, n_group)),
                dma((3, n_group)),
            ],
            compiler_params=pltpu.CompilerParams(
                collective_id=0, has_side_effects=True, vmem_limit_bytes=62 * 1024 * 1024,
            ),
            name="mla_decode",
        )(*operands)
        return out.reshape(n_rows, d_model)

    return jax.shard_map(mla_step, mesh=mesh, in_specs=in_specs, out_specs=row_spec, check_vma=False)
```

time: 133 us -> 49.3 us (0.37)
  waiting for transfers between devices: 51.8 us -> 0 us
  Pallas kernels: 0 us -> 45.9 us
  matrix products: 40.2 us -> 0 us
  blocking collectives: 20.6 us -> 0 us
  between operations: 13.5 us -> 0.01 us
  other arithmetic: 4.06 us -> 0 us
    pallas_call x0 -> x1, Pallas kernels: none -> 45.9 us  [mla_step(): pl.pallas_call(kernel, out_shape=jax.ShapeDtypeStruct((n_group, 8, d_mode...]
    dot_general x6 -> x0, matrix products: 40.2 us -> none  [the longest x1 15.5 us: mla_step(): jnp.einsum('bhc,btc->bht', q_all[:, :, :lat_dim], c_kv, preferred_element...]
    psum x1 -> x0, waiting for transfers between devices: 28.6 us -> none  [mla_step(): y_sum = lax.psum(y_part, 'seq')]
    reduce_scatter x1 -> x0, waiting for transfers between devices: 23.2 us -> none  [mla_step(): merged = lax.psum_scatter(packed, 'seq', scatter_dimension=1, tiled=True)]
    pmax x1 -> x0, blocking collectives: 11 us -> none  [mla_step(): global_max = lax.pmax(local_max, 'seq')]
    all_gather x1 -> x0, blocking collectives: 9.62 us -> none  [mla_step(): q_all = lax.all_gather(q_local, 'seq', axis=1, tiled=True)]
    reduce_sum x1 -> x0, other arithmetic: 2.17 us -> none  [mla_step(): weight_sum = jnp.sum(p_weights, axis=2)]
    reshape x0 -> x2, local copies, waits for them, and re-layouts: none -> 1.66 us  [mla_step(): hid3 = jnp.transpose(hidden.reshape(n_group, 8, 2, half), (2, 0, 1, 3))]
  transfers between devices with their start and end apart: 2 -> 0, of which waited for: 2 -> 0; matrix products, arithmetic and copies ran while one was open for 0% -> 0% of each run, Pallas kernels for 0% -> 0%
where the time goes in v1:
time: 49.3 us; the launch traced here: 49.2 us
  Pallas kernels  45.9 us (93%)
  local copies, waits for them, and re-layouts  3.23 us (7%)
    pallas_call x1, Pallas kernels, mla_step(): pl.pallas_call(kernel, out_shape=jax.ShapeDtypeStruct((n_group, 8, d_mode...  45.9 us
    reshape x2, local copies, waits for them, and re-layouts, mla_step(): hid3 = jnp.transpose(hidden.reshape(n_group, 8, 2, half), (2, 0, 1, 3))  1.66 us
    unnamed x1, local copies, waits for them, and re-layouts  1.57 us

profile of v1, /device:TPU:0, one launch (start us, length us, event | category | flops | bytes accessed | tf_op | source)
XLA Modules:
  0.0 49.2 jit_solution(16511690490215401350)
XLA Ops:
  0.0 1.0 %reshape.18 = bf16[4,8,2,1024]{3,2,1,0:T(2,128)(2,1)S(1)} reshape(bf16[32,2048]{1,0:T(8,128)(2,1)} %hid_hbm.1) | data formatting | bytes 262144 | tf_op jit(solution)/shard_map/reshape | solution.py:328
  1.0 0.7 %copy.12 = bf16[4,8,2,1024]{3,1,0,2:T(8,128)(2,1)} copy(bf16[4,8,2,1024]{3,2,1,0:T(2,128)(2,1)S(1)} %reshape.18) | data formatting | bytes 262144 | tf_op jit(solution)/shard_map/reshape | solution.py:328
  1.7 45.9 %mla_decode.1 = bf16[4,8,2048]{2,1,0:T(8,128)(2,1)} custom-call(s32[32]{0:T(128)} %len_hbm.1, bf16[32,2048]{1,0:T(8,128)(2,1)} %hid_hbm.1, bf16[2,4,8,1024]{3,2,1,0:T(8,128)(2,1)} %bitcast.16, bf16[8192,128]{1,0:T(8,128)(2,1)} %bitcast.12, bf16[256,2048]{1,0:T(8,128)(2,1)} %bitcast.14, bf16[512,512]{1,0:T(8,128)(2,1)} %bitcast.15, ...), custom_call_target="tpu_custom_call" | custom-call | tf_op jit(solution)/shard_map/mla_decode/pallas_call | solution.py:343
  47.6 1.6 %copy.14 = bf16[32,2048]{1,0:T(8,128)(2,1)} copy(bf16[32,2048]{1,0:T(8,128)(2,1)} %bitcast.17) | data formatting | bytes 262144

commit v2 on v1

--- a/solution.py
+++ b/solution.py
@@ -196,7 +196,6 @@
     stat_lane8 = iota((8, STAT), 1) < STAT // 2
 
     def merge_pair(p):
-        pair_copy(p).wait_recv()
         both = []
         for i in (0, 1):
             acc, m, l = merge(acc_src[c, 2 * p + i], r1[2 * p + i])
@@ -207,10 +206,8 @@
             one = jnp.where(upper, both[1][k], both[0][k])
             keep_v[p, :, lo:hi] = jnp.where(x == 0, zero, one)
             s2[p, :, lo:hi] = jnp.where(x == 0, one, zero)
-        chip_copy(p).start()
 
     def o_rows(p):
-        chip_copy(p).wait_recv()
         acc, _, l = merge(keep_v[p], r2[p])
         return acc / l
 
@@ -243,7 +240,7 @@
 
     def y_final(g):
         y_copy(1, g).wait_recv()
-        hid = hid3_v[c, g].astype(F32)
+        hid = hid3_v[g, :, pl.ds(pl.multiple_of(c * half_d, half_d), half_d)].astype(F32)
         f_src[g] = (hid + (yc[g] + yr2[g])).astype(BF16)
         y_copy(2, g).start()
 
@@ -253,45 +250,80 @@
         out_ref[g, :, 0:half_d] = jnp.where(c == 0, mine, other).astype(BF16)
         out_ref[g, :, half_d:d_model] = jnp.where(c == 0, other, mine).astype(BF16)
 
-    def step(j, carry, with_merge):
+    def wait_group(g):
+        for i in range(GROUP):
+            chip_copy(GROUP * g + i).wait_recv()
+
+    def step(j, with_merge, group=None):
         wait_rows(j)
+        if with_merge:
+            pair_copy(j - GROUP).wait_recv()
+        if group is not None:
+            wait_group(group)
         scores(j)
         attend(j - 1)
+        if with_merge:
+            merge_pair(j - GROUP)
+        if group is not None:
+            project(group)
         pair_copy(j - 1).start()
         if with_merge:
-            merge_pair(j - GROUP)
-        return carry
-
-    for g in range(n_group):
+            chip_copy(j - GROUP).start()
+        if group is not None:
+            y_copy(0, group).start()
+
+    def steps(lo, hi, with_merge):
+        def body(j, carry):
+            step(j, with_merge)
+            return carry
+
+        lax.fori_loop(lo, hi, body, 0)
+
+    def forward(g):
         q_copy(1, g).wait_recv()
         q_copy(2, g).start()
+
+    forward(0)
+    for g in range(n_group):
+        first, last = GROUP * g, GROUP * (g + 1)
         q_copy(0, g).wait_recv()
         q_copy(2, g).wait_recv()
         if g == 0:
             wait_rows(0)
             scores(0)
-        lax.fori_loop(max(1, GROUP * g), GROUP * (g + 1), lambda j, cy, m=g > 0: step(j, cy, m), 0)
+            first += 1
         if g == 2:
             for w in late_weights:
                 w.wait()
         if g >= 2:
-            project(g - 2)
-            y_copy(0, g - 2).start()
+            step(first, True, g - 2)
+            first += 1
+        steps(first, GROUP * g + 2, g > 0)
+        if g + 1 < n_group:
+            forward(g + 1)
         if g >= 3:
             y_chip(g - 3)
+        steps(GROUP * g + 2, last, g > 0)
+    for p in range(n_pair - GROUP, n_pair - 1):
+        pair_copy(p).wait_recv()
+    wait_group(n_group - 2)
     attend(n_pair - 1)
     pair_copy(n_pair - 1).start()
     for p in range(n_pair - GROUP, n_pair - 1):
         merge_pair(p)
-    for g in range(n_group - 2, n_group):
-        if g == n_group - 1:
-            merge_pair(n_pair - 1)
-            y_chip(n_group - 3)
-            y_chip(n_group - 2)
-            y_final(n_group - 4)
-        project(g)
-        y_copy(0, g).start()
+        chip_copy(p).start()
+    y_chip(n_group - 3)
+    y_final(n_group - 4)
+    project(n_group - 2)
+    y_copy(0, n_group - 2).start()
+    pair_copy(n_pair - 1).wait_recv()
+    merge_pair(n_pair - 1)
+    chip_copy(n_pair - 1).start()
+    y_chip(n_group - 2)
     y_final(n_group - 3)
+    wait_group(n_group - 1)
+    project(n_group - 1)
+    y_copy(0, n_group - 1).start()
     y_final(n_group - 2)
     y_chip(n_group - 1)
     y_final(n_group - 1)
@@ -325,7 +357,7 @@
         n_group = n_pair // GROUP
         wide = lat + STAT
         half = d_model // 2
-        hid3 = jnp.transpose(hidden.reshape(n_group, 8, 2, half), (2, 0, 1, 3))
+        hid3 = hidden.reshape(n_group, 8, d_model)
         operands = (
             lengths,
             hidden,
@@ -338,6 +370,7 @@
             c_kv,
             jnp.transpose(k_rope, (0, 2, 1)),
         )
+        operands = tuple(pltpu.with_memory_space_constraint(a, pltpu.HBM) for a in operands)
         vm = pltpu.VMEM
         dma = pltpu.SemaphoreType.DMA
         out = pl.pallas_call(
@@ -383,7 +416,7 @@
                 dma((3, n_group)),
             ],
             compiler_params=pltpu.CompilerParams(
-                collective_id=0, has_side_effects=True, vmem_limit_bytes=62 * 1024 * 1024,
+                collective_id=0, has_side_effects=True, vmem_limit_bytes=50 * 1024 * 1024,
             ),
             name="mla_decode",
         )(*operands)

time: 49.3 us -> 46.9 us (0.951)
  local copies, waits for them, and re-layouts: 3.23 us -> 0.66 us
    reshape x2 -> x0, local copies, waits for them, and re-layouts: 1.66 us -> none  [mla_step(): hid3 = jnp.transpose(hidden.reshape(n_group, 8, 2, half), (2, 0, 1, 3))]
    unnamed x1, local copies, waits for them, and re-layouts: 1.57 us -> 0.66 us
where the time goes in v2:
time: 46.9 us; the launch traced here: 46.8 us
  Pallas kernels  46.1 us (98%)
  local copies, waits for them, and re-layouts  0.66 us (1%)
    pallas_call x1, Pallas kernels, mla_step(): pl.pallas_call(kernel, out_shape=jax.ShapeDtypeStruct((n_group, 8, d_mode...  46.1 us

profile of v2, /device:TPU:0, one launch (start us, length us, event | category | flops | bytes accessed | tf_op | source)
XLA Modules:
  0.0 46.8 jit_solution(10901854698859422946)
XLA Ops:
  0.0 46.1 %mla_decode.1 = bf16[4,8,2048]{2,1,0:T(8,128)(2,1)S(1)} custom-call(s32[32]{0:T(128)} %len_hbm.1, bf16[32,2048]{1,0:T(8,128)(2,1)} %hid_hbm.1, bf16[4,8,2048]{2,1,0:T(8,128)(2,1)} %bitcast.15, bf16[8192,128]{1,0:T(8,128)(2,1)} %bitcast.11, bf16[256,2048]{1,0:T(8,128)(2,1)} %bitcast.13, bf16[512,512]{1,0:T(8,128)(2,1)} %bitcast.14, ...), custom_call_target="tpu_custom_call" | custom-call | tf_op jit(solution)/shard_map/mla_decode/pallas_call | solution.py:376
  46.1 0.7 %copy.11 = bf16[32,2048]{1,0:T(8,128)(2,1)} copy(bf16[32,2048]{1,0:T(8,128)(2,1)S(1)} %bitcast.9) | data formatting | bytes 262144

commit v3 on v1

--- a/solution.py
+++ b/solution.py
@@ -49,45 +49,52 @@
     c = lax.rem(me, 2)
     sib = 2 * x + (1 - c)
     cnt = 2 * (1 - x) + c
+    far = 3 - me
 
     def load(src, dst, sem):
         return pltpu.make_async_copy(src, dst, sem)
 
-    weights = [
-        load(hid_hbm, hid_v, w_sem.at[0]),
-        load(wuq_hbm, wuq_v, w_sem.at[1]),
-        load(wqr_hbm, wqr_v, w_sem.at[2]),
-        load(wuk_hbm, wuk_v, w_sem.at[3]),
-        load(len_hbm, len_s, w_sem.at[4]),
-        load(hid3_hbm, hid3_v, w_sem.at[5]),
-    ]
-    late_weights = [
-        load(wuv_hbm, wuv_v, w_sem.at[6]),
-        load(wo_hbm, wo_v, w_sem.at[7]),
-    ]
-
-    def ckv_load(b):
-        return load(ckv_hbm.at[b], ckv_v.at[b], ckv_sem.at[b])
-
-    def kr_load(b):
-        return load(kr_hbm.at[b], kr_v.at[b], kr_sem.at[b])
-
-    for w in weights:
+    loads = {
+        "hid": load(hid_hbm, hid_v, w_sem.at[0]),
+        "wqr": load(wqr_hbm, wqr_v, w_sem.at[1]),
+        "wuk": load(wuk_hbm, wuk_v, w_sem.at[2]),
+        "len": load(len_hbm, len_s, w_sem.at[7]),
+        "hid3": load(hid3_hbm, hid3_v, w_sem.at[8]),
+    }
+    n_part = 4
+    part = wuq_hbm.shape[0] // n_part
+    for i in range(n_part):
+        rows = pl.ds(i * part, part)
+        loads["wuq", i] = load(wuq_hbm.at[rows], wuq_v.at[rows], w_sem.at[3 + i])
+    late = {
+        "wuv": load(wuv_hbm, wuv_v, w_sem.at[9]),
+        "wo": load(wo_hbm, wo_v, w_sem.at[10]),
+    }
+
+    def ckv_load(p):
+        rows = pl.ds(2 * p, 2)
+        return load(ckv_hbm.at[rows], ckv_v.at[rows], ckv_sem.at[p])
+
+    def kr_load(p):
+        rows = pl.ds(2 * p, 2)
+        return load(kr_hbm.at[rows], kr_v.at[rows], kr_sem.at[p])
+
+    for w in loads.values():
         w.start()
 
     barrier = pltpu.get_barrier_semaphore()
-    for peer in (sib, cnt):
+    for peer in (sib, cnt, far):
         pl.semaphore_signal(barrier, inc=1, device_id={"seq": peer}, device_id_type=MESH)
 
-    def start_rows(b, carry):
-        kr_load(b).start()
-        ckv_load(b).start()
+    def start_rows(p, carry):
+        kr_load(p).start()
+        ckv_load(p).start()
         return carry
 
-    lax.fori_loop(0, n_rows // 2, start_rows, 0)
-    for w in late_weights:
+    lax.fori_loop(0, n_pair // 2, start_rows, 0)
+    for w in late.values():
         w.start()
-    lax.fori_loop(n_rows // 2, n_rows, start_rows, 0)
+    lax.fori_loop(n_pair // 2, n_pair, start_rows, 0)
 
     def remote(src, dst, send, recv, peer):
         return pltpu.make_async_remote_copy(
@@ -99,29 +106,19 @@
     n_local = n_rows * n_head
     lane_h = iota((n_rows, 4 * nope), 1) % n_head
     spread = (iota((nope, n_head * nope), 1) // n_head == iota((nope, n_head * nope), 0)).astype(F32).astype(BF16)
-    for i in (0, 1):
-        weights[i].wait()
+    loads["hid"].wait()
     for k in range(d_model // nope):
         wide = dot(hid_v[:, k * nope:(k + 1) * nope], spread)
         for h in range(n_head):
             em_v[h * n_rows:(h + 1) * n_rows, k * n_head * nope:(k + 1) * n_head * nope] = jnp.where(
                 lane_h == h, wide, 0.0).astype(BF16)
-    q_n = dot(em_v[...], wuq_v[...]).astype(BF16)
-    for i in (2, 3, 4, 5):
-        weights[i].wait()
-    q_r = dot_t(hid_v[...], wqr_v[...]).astype(BF16)
 
     def row_of(r):
         j = (r // 4) % 2
         return 2 * (r // 8) + j + x - 2 * j * x
 
-    r_id = iota((n_local, n_local), 0)
-    col = iota((n_local, n_local), 1)
-    perm = (col == (r_id % 4) * n_rows + row_of(r_id)).astype(F32).astype(BF16)
-    q_p = dot(perm, q_n)
-    r_h = iota((n_local, nope), 0) % 4
-    q_wide = jnp.concatenate([jnp.where(r_h == h, q_p, 0.0).astype(BF16) for h in range(n_head)], axis=1)
-    q_l = dot(q_wide, wuk_v[...]).astype(BF16)
+    loads["wqr"].wait()
+    q_r = dot_t(hid_v[...], wqr_v[...]).astype(BF16)
     r_id = iota((n_local, n_rows), 0)
     rep = (iota((n_local, n_rows), 1) == row_of(r_id)).astype(F32).astype(BF16)
     q_r = dot(rep, q_r)
@@ -129,20 +126,43 @@
     fold = (iota((n_head * rope, STAT), 0) % rope == iota((n_head * rope, STAT), 1)).astype(F32).astype(BF16)
     q_r = dot(q_r.astype(BF16), fold).astype(BF16)
     for p in range(n_pair):
+        qall[me, p, :, lat:lat + STAT] = q_r[8 * p:8 * p + 8]
+    r_id = iota((n_local, n_local), 0)
+    col = iota((n_local, n_local), 1)
+    perm = (col == (r_id % 4) * n_rows + row_of(r_id)).astype(F32).astype(BF16)
+    r_h = iota((n_local, nope), 0) % 4
+
+    for name in ("wuk", "len", "hid3"):
+        loads[name].wait()
+    for i in range(n_part):
+        loads["wuq", i].wait()
+        rows = slice(i * part, (i + 1) * part)
+        term = dot(em_v[:, rows], wuq_v[rows, :])
+        q_n = term if i == 0 else q_n + term
+    q_p = dot(perm, q_n.astype(BF16))
+    q_wide = jnp.concatenate([jnp.where(r_h == h, q_p, 0.0).astype(BF16) for h in range(n_head)], axis=1)
+    q_l = dot(q_wide, wuk_v[...]).astype(BF16)
+    for p in range(n_pair):
         qall[me, p, :, 0:lat] = q_l[8 * p:8 * p + 8]
-        qall[me, p, :, lat:lat + STAT] = q_r[8 * p:8 * p + 8]
-
-    pl.semaphore_wait(barrier, 2)
+
+    pl.semaphore_wait(barrier, 3)
+
+    chunks = ((0, 3), (3, 7), (7, n_pair))
 
     def q_copy(kind, g):
-        slot, peer = ((me, sib), (me, cnt), (cnt, sib))[kind]
-        part = qall.at[slot, pl.ds(GROUP * g, GROUP)]
-        return remote(part, part, q_send.at[kind, g], q_recv.at[kind, g], peer)
-
-    for g in range(n_group):
-        q_copy(1, g).start()
-    for g in range(n_group):
-        q_copy(0, g).start()
+        slot, peer = ((me, sib), (me, cnt), (me, far) if g == 0 else (cnt, sib))[kind]
+        first, last = chunks[g]
+        rows = qall.at[slot, first:last]
+        return remote(rows, rows, q_send.at[kind], q_recv.at[kind, g], peer)
+
+    def q_forward(g):
+        q_copy(1, g).wait_recv()
+        q_copy(2, g).start()
+
+    for kind in (1, 2, 0):
+        q_copy(kind, 0).start()
+    q_copy(1, 1).start()
+    q_copy(0, 1).start()
 
     upper8 = iota((8, lat + STAT), 0) < 4
 
@@ -157,9 +177,8 @@
             sbuf[p % 2, i] = s
 
     def wait_rows(p):
-        for i in (0, 1):
-            kr_load(2 * p + i).wait()
-            ckv_load(2 * p + i).wait()
+        kr_load(p).wait()
+        ckv_load(p).wait()
 
     stat_lane = iota((16, STAT), 1) < STAT // 2
 
@@ -180,10 +199,10 @@
 
     def pair_copy(p):
         rows = pl.ds(2 * p, 2)
-        return remote(acc_src.at[1 - c, rows], r1.at[rows], a_send.at[p], a_recv.at[p], sib)
+        return remote(acc_src.at[1 - c, rows], r1.at[rows], a_send, a_recv.at[p], sib)
 
     def chip_copy(p):
-        return remote(s2.at[p], r2.at[p], c_send.at[p], c_recv.at[p], cnt)
+        return remote(s2.at[p], r2.at[p], c_send, c_recv.at[p], cnt)
 
     def merge(a, b):
         m1, l1 = a[:, lat:lat + 1], a[:, lat + STAT // 2:lat + STAT // 2 + 1]
@@ -196,7 +215,6 @@
     stat_lane8 = iota((8, STAT), 1) < STAT // 2
 
     def merge_pair(p):
-        pair_copy(p).wait_recv()
         both = []
         for i in (0, 1):
             acc, m, l = merge(acc_src[c, 2 * p + i], r1[2 * p + i])
@@ -207,10 +225,8 @@
             one = jnp.where(upper, both[1][k], both[0][k])
             keep_v[p, :, lo:hi] = jnp.where(x == 0, zero, one)
             s2[p, :, lo:hi] = jnp.where(x == 0, one, zero)
-        chip_copy(p).start()
 
     def o_rows(p):
-        chip_copy(p).wait_recv()
         acc, _, l = merge(keep_v[p], r2[p])
         return acc / l
 
@@ -234,7 +250,7 @@
             src, dst, peer = yc.at[g], yr2.at[g], cnt
         else:
             src, dst, peer = f_src.at[g], f_rcv.at[g], sib
-        return remote(src, dst, y_send.at[kind, g], y_recv.at[kind, g], peer)
+        return remote(src, dst, y_send.at[kind], y_recv.at[kind, g], peer)
 
     def y_chip(g):
         y_copy(0, g).wait_recv()
@@ -243,7 +259,7 @@
 
     def y_final(g):
         y_copy(1, g).wait_recv()
-        hid = hid3_v[c, g].astype(F32)
+        hid = hid3_v[g, :, pl.ds(pl.multiple_of(c * half_d, half_d), half_d)].astype(F32)
         f_src[g] = (hid + (yc[g] + yr2[g])).astype(BF16)
         y_copy(2, g).start()
 
@@ -253,62 +269,89 @@
         out_ref[g, :, 0:half_d] = jnp.where(c == 0, mine, other).astype(BF16)
         out_ref[g, :, half_d:d_model] = jnp.where(c == 0, other, mine).astype(BF16)
 
-    def step(j, carry, with_merge):
-        wait_rows(j)
-        scores(j)
-        attend(j - 1)
-        pair_copy(j - 1).start()
-        if with_merge:
-            merge_pair(j - GROUP)
-        return carry
-
-    for g in range(n_group):
-        q_copy(1, g).wait_recv()
-        q_copy(2, g).start()
-        q_copy(0, g).wait_recv()
-        q_copy(2, g).wait_recv()
-        if g == 0:
-            wait_rows(0)
-            scores(0)
-        lax.fori_loop(max(1, GROUP * g), GROUP * (g + 1), lambda j, cy, m=g > 0: step(j, cy, m), 0)
-        if g == 2:
-            for w in late_weights:
-                w.wait()
-        if g >= 2:
-            project(g - 2)
-            y_copy(0, g - 2).start()
-        if g >= 3:
-            y_chip(g - 3)
+    def step(js, merges=(), groups=()):
+        for j in js:
+            wait_rows(j)
+        for p in merges:
+            pair_copy(p).wait_recv()
+        for g in groups:
+            for i in range(GROUP):
+                chip_copy(GROUP * g + i).wait_recv()
+        for j in js:
+            scores(j)
+            attend(j - 1)
+        for p in merges:
+            merge_pair(p)
+        for g in groups:
+            project(g)
+        for j in js:
+            pair_copy(j - 1).start()
+        for p in merges:
+            chip_copy(p).start()
+        for g in groups:
+            y_copy(0, g).start()
+
+    for kind in range(3):
+        q_copy(kind, 0).wait_recv()
+    q_copy(1, 2).start()
+    q_copy(0, 2).start()
+    wait_rows(0)
+    scores(0)
+    q_forward(1)
+    step((1, 2))
+    q_copy(0, 1).wait_recv()
+    q_copy(2, 1).wait_recv()
+    step((3, 4))
+    q_forward(2)
+    step((5, 6), (0, 1))
+    q_copy(0, 2).wait_recv()
+    q_copy(2, 2).wait_recv()
+    step((7, 8), (2, 3))
+    step((9, 10), (4, 5))
+    step((11,), (6, 7))
+    for w in late.values():
+        w.wait()
+    step((12,), (8, 9), (0,))
+    step((13,), (10,))
+    y_chip(0)
+    step((14,), (11,))
+    step((15,), (12,), (1,))
     attend(n_pair - 1)
     pair_copy(n_pair - 1).start()
-    for p in range(n_pair - GROUP, n_pair - 1):
+
+    def last_merge(p):
+        pair_copy(p).wait_recv()
         merge_pair(p)
-    for g in range(n_group - 2, n_group):
-        if g == n_group - 1:
-            merge_pair(n_pair - 1)
-            y_chip(n_group - 3)
-            y_chip(n_group - 2)
-            y_final(n_group - 4)
+        chip_copy(p).start()
+
+    def last_project(g):
+        for i in range(GROUP):
+            chip_copy(GROUP * g + i).wait_recv()
         project(g)
         y_copy(0, g).start()
-    y_final(n_group - 3)
-    y_final(n_group - 2)
-    y_chip(n_group - 1)
-    y_final(n_group - 1)
-    for g in range(n_group):
-        store(g)
-
-    for g in range(n_group):
-        for kind in range(3):
-            q_copy(kind, g).wait_send()
-            y_copy(kind, g).wait_send()
-
-    def drain(p, carry):
-        pair_copy(p).wait_send()
-        chip_copy(p).wait_send()
-        return carry
-
-    lax.fori_loop(0, n_pair, drain, 0)
+
+    last_merge(13)
+    last_merge(14)
+    last_merge(15)
+    y_chip(1)
+    y_final(0)
+    last_project(2)
+    y_chip(2)
+    last_project(3)
+    y_final(1)
+    y_chip(3)
+    store(0)
+    y_final(2)
+    store(1)
+    store(2)
+    y_final(3)
+    for kind in range(3):
+        remote(qall.at[me], qall.at[me], q_send.at[kind], q_recv.at[kind, 0], sib).wait_send()
+        whole = (yr1, yr2, f_rcv)[kind]
+        remote(whole, whole, y_send.at[kind], y_recv.at[kind, 0], sib).wait_send()
+    remote(r1, r1, a_send, a_recv.at[0], sib).wait_send()
+    remote(r2, r2, c_send, c_recv.at[0], cnt).wait_send()
+    store(3)
 
 
 def solution(mesh):
@@ -325,7 +368,7 @@
         n_group = n_pair // GROUP
         wide = lat + STAT
         half = d_model // 2
-        hid3 = jnp.transpose(hidden.reshape(n_group, 8, 2, half), (2, 0, 1, 3))
+        hid3 = hidden.reshape(n_group, 8, d_model)
         operands = (
             lengths,
             hidden,
@@ -338,6 +381,7 @@
             c_kv,
             jnp.transpose(k_rope, (0, 2, 1)),
         )
+        operands = tuple(pltpu.with_memory_space_constraint(a, pltpu.HBM) for a in operands)
         vm = pltpu.VMEM
         dma = pltpu.SemaphoreType.DMA
         out = pl.pallas_call(
@@ -370,20 +414,20 @@
                 vm((n_group, 8, half), F32),
                 vm((n_group, 8, half), BF16),
                 vm((n_group, 8, half), BF16),
-                dma((8,)),
-                dma((n_rows,)),
-                dma((n_rows,)),
-                dma((3, n_group)),
-                dma((3, n_group)),
+                dma((11,)),
                 dma((n_pair,)),
                 dma((n_pair,)),
+                dma((3,)),
+                dma((3, 3)),
+                dma(()),
                 dma((n_pair,)),
+                dma(()),
                 dma((n_pair,)),
-                dma((3, n_group)),
+                dma((3,)),
                 dma((3, n_group)),
             ],
             compiler_params=pltpu.CompilerParams(
-                collective_id=0, has_side_effects=True, vmem_limit_bytes=62 * 1024 * 1024,
+                collective_id=0, has_side_effects=True, vmem_limit_bytes=50 * 1024 * 1024,
             ),
             name="mla_decode",
         )(*operands)

time: 49.3 us -> 36.8 us (0.75)
  Pallas kernels: 45.9 us -> 36.1 us
  local copies, waits for them, and re-layouts: 3.23 us -> 0.66 us
    pallas_call x1, Pallas kernels: 45.9 us -> 36.1 us  [mla_step(): pl.pallas_call(kernel, out_shape=jax.ShapeDtypeStruct((n_group, 8, d_mode...]
    reshape x2 -> x0, local copies, waits for them, and re-layouts: 1.66 us -> none  [mla_step(): hid3 = jnp.transpose(hidden.reshape(n_group, 8, 2, half), (2, 0, 1, 3))]
    unnamed x1, local copies, waits for them, and re-layouts: 1.57 us -> 0.66 us
where the time goes in v3:
time: 36.8 us; the launch traced here: 36.7 us
  Pallas kernels  36.1 us (98%)
  local copies, waits for them, and re-layouts  0.66 us (2%)
    pallas_call x1, Pallas kernels, mla_step(): pl.pallas_call(kernel, out_shape=jax.ShapeDtypeStruct((n_group, 8, d_mode...  36.1 us

profile of v3, /device:TPU:0, one launch (start us, length us, event | category | flops | bytes accessed | tf_op | source)
XLA Modules:
  0.0 36.7 jit_solution(8297563479740113930)
XLA Ops:
  0.0 36.1 %mla_decode.1 = bf16[4,8,2048]{2,1,0:T(8,128)(2,1)S(1)} custom-call(s32[32]{0:T(128)} %len_hbm.1, bf16[32,2048]{1,0:T(8,128)(2,1)} %hid_hbm.1, bf16[4,8,2048]{2,1,0:T(8,128)(2,1)} %bitcast.15, bf16[8192,128]{1,0:T(8,128)(2,1)} %bitcast.11, bf16[256,2048]{1,0:T(8,128)(2,1)} %bitcast.13, bf16[512,512]{1,0:T(8,128)(2,1)} %bitcast.14, ...), custom_call_target="tpu_custom_call" | custom-call | tf_op jit(solution)/shard_map/mla_decode/pallas_call | solution.py:387
  36.1 0.7 %copy.11 = bf16[32,2048]{1,0:T(8,128)(2,1)} copy(bf16[32,2048]{1,0:T(8,128)(2,1)S(1)} %bitcast.9) | data formatting | bytes 262144

commit v4 on v3

v4 whole, which is shorter than its diff:
```python
import math

import jax
import jax.numpy as jnp
from jax import lax
from jax.experimental import pallas as pl
from jax.experimental.pallas import tpu as pltpu
from jax.sharding import PartitionSpec as P

MESH = pl.DeviceIdType.MESH
F32 = jnp.float32
BF16 = jnp.bfloat16
GROUP = 4
STAT = 128


def dot(a, b):
    return jnp.dot(a, b, preferred_element_type=F32)


def dot_t(a, b):
    return lax.dot_general(a, b, (((1,), (1,)), ((), ())), preferred_element_type=F32)


def iota(shape, dim):
    return lax.broadcasted_iota(jnp.int32, shape, dim)


def kernel(
    len_hbm, hid_hbm, hid3_hbm, wuq_hbm, wqr_hbm, wuk_hbm, wuv_hbm, wo_hbm, ckv_hbm, kr_hbm,
    out_ref,
    len_s, hid_v, hid3_v, hid_r, wuq_v, wqr_v, wuk_v, wuv_v, wo_v, ckv_v, kr_v,
    em_v, qall, sbuf, acc_src, r1, s2, keep_v, r2, y_src, yr1, yc, yr2, f_src, f_rcv, y_last,
    w_sem, ckv_sem, kr_sem, q_send, q_recv, a_send, a_recv, c_send, c_recv, y_send, y_recv, f_send, f_recv, l_send, l_recv,
):
    n_rows = ckv_hbm.shape[0]
    shard = ckv_hbm.shape[1]
    lat = ckv_hbm.shape[2]
    rope = kr_hbm.shape[1]
    nope = wuq_hbm.shape[1]
    n_pair = n_rows // 2
    n_group = n_pair // GROUP
    d_model = hid_hbm.shape[1]
    half_d = d_model // 2
    scale = 1.0 / math.sqrt(nope + rope)

    me = lax.axis_index("seq")
    x = lax.div(me, 2)
    c = lax.rem(me, 2)
    sib = 2 * x + (1 - c)
    cnt = 2 * (1 - x) + c
    far = 3 - me

    def load(src, dst, sem):
        return pltpu.make_async_copy(src, dst, sem)

    hid_load = load(hid_hbm, hid_v, w_sem.at[0])
    early = [load(src, dst, w_sem.at[1 + i]) for i, (src, dst) in enumerate((
        (wqr_hbm, wqr_v), (wuk_hbm, wuk_v), (len_hbm, len_s), (hid3_hbm, hid3_v), (wuq_hbm, wuq_v)))]
    late = [load(src, dst, w_sem.at[6 + i]) for i, (src, dst) in enumerate(((wuv_hbm, wuv_v), (wo_hbm, wo_v)))]
    spans = ((0, 1), (1, 3), (3, 7), (7, 11), (11, n_pair))

    def row_loads(i):
        rows = slice(2 * spans[i][0], 2 * spans[i][1])
        return (load(kr_hbm.at[rows], kr_v.at[rows], kr_sem.at[i]), load(ckv_hbm.at[rows], ckv_v.at[rows], ckv_sem.at[i]))

    for w in (hid_load, *early):
        w.start()

    barrier = pltpu.get_barrier_semaphore()
    for peer in (sib, cnt, far):
        pl.semaphore_signal(barrier, inc=1, device_id={"seq": peer}, device_id_type=MESH)

    for i in range(len(spans)):
        for w in row_loads(i):
            w.start()
        if i == 2:
            for w in late:
                w.start()

    def remote(src, dst, send, recv, peer):
        return pltpu.make_async_remote_copy(
            src_ref=src, dst_ref=dst, send_sem=send, recv_sem=recv,
            device_id={"seq": peer}, device_id_type=MESH,
        )

    n_head = wqr_hbm.shape[0] // rope
    n_local = n_rows * n_head
    def row_of(r):
        j = (r // 4) % 2
        return 2 * (r // 8) + j + x - 2 * j * x

    r_h = iota((n_local, nope), 0) % 4
    same_head = iota((n_local, n_head * nope), 1) % n_head == iota((n_local, n_head * nope), 0) % 4
    spread = (iota((nope, n_head * nope), 1) // n_head == iota((nope, n_head * nope), 0)).astype(F32).astype(BF16)
    rep = (iota((n_local, n_rows), 1) == row_of(iota((n_local, n_rows), 0))).astype(F32).astype(BF16)
    fold = (iota((n_head * rope, STAT), 0) % rope == iota((n_head * rope, STAT), 1)).astype(F32).astype(BF16)
    hid_load.wait()
    hid_r[...] = dot(rep, hid_v[...]).astype(BF16)
    for k in range(d_model // nope):
        wide = dot(hid_r[:, k * nope:(k + 1) * nope], spread)
        em_v[:, k * n_head * nope:(k + 1) * n_head * nope] = jnp.where(same_head, wide, 0.0).astype(BF16)
    for w in early:
        w.wait()
    q_r = dot_t(hid_r[...], wqr_v[...])
    q_n = dot(em_v[...], wuq_v[...])
    q_r = jnp.where(iota((n_local, n_head * rope), 1) // rope == iota((n_local, n_head * rope), 0) % 4, q_r, 0.0)
    q_r = dot(q_r.astype(BF16), fold).astype(BF16)
    q_wide = jnp.concatenate([jnp.where(r_h == h, q_n, 0.0).astype(BF16) for h in range(n_head)], axis=1)
    q_l = dot(q_wide, wuk_v[...]).astype(BF16)
    for p in range(n_pair):
        qall[me, p, :, 0:lat] = q_l[8 * p:8 * p + 8]
        qall[me, p, :, lat:lat + STAT] = q_r[8 * p:8 * p + 8]

    pl.semaphore_wait(barrier, 3)

    chunks = ((0, 1), (1, 3), (3, 7), (7, n_pair))
    last_chunk = len(chunks) - 1

    def q_copy(kind, g):
        forward = g == last_chunk and kind == 1
        slot, peer = ((me, cnt), (cnt, sib) if forward else (me, far), (me, sib))[kind]
        rows = qall.at[slot, chunks[g][0]:chunks[g][1]]
        return remote(rows, rows, q_send, q_recv.at[g + 1 if g == last_chunk and kind == 0 else g], peer)

    def q_wait(g):
        rows = qall.at[0:2 if g == last_chunk else 3, chunks[g][0]:chunks[g][1]]
        remote(rows, rows, q_send, q_recv.at[g], sib).wait_recv()

    for g in range(last_chunk):
        for kind in range(3):
            q_copy(kind, g).start()

    upper8 = iota((8, lat + STAT), 0) < 4

    def scores(p):
        tiles = [qall[s, p].astype(F32) for s in range(4)]
        q_even = jnp.concatenate([jnp.where(upper8, tiles[0], tiles[2]), jnp.where(upper8, tiles[1], tiles[3])], axis=0)
        q_odd = jnp.concatenate([jnp.where(upper8, tiles[2], tiles[0]), jnp.where(upper8, tiles[3], tiles[1])], axis=0)
        for i, q in enumerate((q_even, q_odd)):
            q = q.astype(BF16)
            b = 2 * p + i
            s = dot_t(q[:, :lat], ckv_v[b]) + dot(q[:, lat:lat + rope], kr_v[b])
            sbuf[p % 2, i] = s

    def wait_rows(p):
        for i, span in enumerate(spans):
            if p == span[0]:
                for w in row_loads(i):
                    w.wait()

    stat_lane = iota((16, STAT), 1) < STAT // 2

    def attend(p):
        for i in (0, 1):
            b = 2 * p + i
            s = sbuf[p % 2, i] * scale
            pos = me * shard + iota(s.shape, 1)
            s = jnp.where(pos < len_s[b], s, -jnp.inf)
            m = jnp.max(s, axis=1, keepdims=True)
            e = jnp.exp(s - jnp.where(m > -jnp.inf, m, 0.0))
            l = jnp.sum(e, axis=1, keepdims=True)
            acc = dot(e.astype(BF16), ckv_v[b])
            stat = jnp.where(stat_lane, m, l)
            for k in (0, 1):
                acc_src[k, b, :, 0:lat] = acc[8 * k:8 * k + 8]
                acc_src[k, b, :, lat:lat + STAT] = stat[8 * k:8 * k + 8]

    sends = ((0, 1), (2, 3), (4, 5), (6, 7), (8, 9), (10,), (11,), (12,), (13,), (14,), (15,))

    def pair_copy(ps):
        rows = slice(2 * ps[0], 2 * ps[-1] + 2)
        return remote(acc_src.at[1 - c, rows], r1.at[rows], a_send, a_recv.at[sends.index(ps)], sib)

    def chip_copy(ps):
        rows = slice(ps[0], ps[-1] + 1)
        return remote(s2.at[rows], r2.at[rows], c_send, c_recv.at[ps[0] // GROUP], cnt)

    def chip_wait(g):
        rows = r2.at[GROUP * g:GROUP * (g + 1)]
        remote(rows, rows, c_send, c_recv.at[g], cnt).wait_recv()

    def merge(a, b):
        m1, l1 = a[:, lat:lat + 1], a[:, lat + STAT // 2:lat + STAT // 2 + 1]
        m2, l2 = b[:, lat:lat + 1], b[:, lat + STAT // 2:lat + STAT // 2 + 1]
        m = jnp.maximum(m1, m2)
        shift = jnp.where(m > -jnp.inf, m, 0.0)
        w1, w2 = jnp.exp(m1 - shift), jnp.exp(m2 - shift)
        return w1 * a[:, :lat] + w2 * b[:, :lat], m, w1 * l1 + w2 * l2

    stat_lane8 = iota((8, STAT), 1) < STAT // 2

    def merge_pair(p):
        both = []
        for i in (0, 1):
            acc, m, l = merge(acc_src[c, 2 * p + i], r1[2 * p + i])
            both.append((acc, jnp.where(stat_lane8, m, l)))
        for k, (lo, hi) in enumerate(((0, lat), (lat, lat + STAT))):
            upper = upper8[:, lo:hi]
            zero = jnp.where(upper, both[0][k], both[1][k])
            one = jnp.where(upper, both[1][k], both[0][k])
            keep_v[p, :, lo:hi] = jnp.where(x == 0, zero, one)
            s2[p, :, lo:hi] = jnp.where(x == 0, one, zero)

    def o_rows(p):
        acc, _, l = merge(keep_v[p], r2[p])
        return acc / l

    n_out = 8 * GROUP

    def project(g):
        o_lat = jnp.concatenate([o_rows(GROUP * g + i) for i in range(GROUP)], axis=0).astype(BF16)
        head = iota((n_out, nope), 0) % 4
        wide = []
        for h in range(0, n_head, 2):
            two = dot(o_lat, jnp.concatenate([wuv_v[h], wuv_v[h + 1]], axis=1))
            wide += [jnp.where(head == h + i, two[:, i * nope:(i + 1) * nope], 0.0).astype(BF16) for i in (0, 1)]
        wide = jnp.concatenate(wide, axis=1)
        r = iota((8, n_out), 1)
        gather = (iota((8, n_out), 0) == row_of(r)).astype(F32).astype(BF16)
        o_val = dot(gather, wide).astype(BF16)
        for k in (0, 1):
            y_src[g, k] = dot(o_val, wo_v[:, k * half_d:(k + 1) * half_d])

    def y_copy(kind, g):
        if kind == 0:
            return remote(y_src.at[g, 1 - c], yr1.at[g], y_send, y_recv.at[0, g], sib)
        return remote(yc.at[g], yr2.at[g], y_send, y_recv.at[1, g], cnt)

    def f_copy(g):
        return remote(f_src.at[g], f_rcv.at[g], f_send, f_recv, sib)

    def last_copy(i):
        return remote(yc.at[n_group - 1], y_last.at[i], l_send, l_recv, (sib, far)[i])

    def y_chip(g):
        y_copy(0, g).wait_recv()
        yc[g] = y_src[g, c] + yr1[g]
        y_copy(1, g).start()

    def hid_half(g, k):
        return hid3_v[g, :, pl.ds(pl.multiple_of(k * half_d, half_d), half_d)].astype(F32)

    def y_final(g):
        y_copy(1, g).wait_recv()
        f_src[g] = (hid_half(g, c) + (yc[g] + yr2[g])).astype(BF16)
        f_copy(g).start()

    def put(g, mine, other):
        out_ref[g, :, 0:half_d] = jnp.where(c == 0, mine, other).astype(BF16)
        out_ref[g, :, half_d:d_model] = jnp.where(c == 0, other, mine).astype(BF16)

    def step(js, merges=(), groups=()):
        for j in js:
            wait_rows(j)
        if merges:
            pair_copy(merges).wait_recv()
        for g in groups:
            chip_wait(g)
        for j in js:
            scores(j)
            attend(j - 1)
        for p in merges:
            merge_pair(p)
        for g in groups:
            project(g)
        pair_copy(tuple(j - 1 for j in js)).start()
        if merges:
            chip_copy(merges).start()
        for g in groups:
            y_copy(0, g).start()

    q_wait(0)
    for kind in (0, 2):
        q_copy(kind, last_chunk).start()
    wait_rows(0)
    scores(0)
    q_wait(1)
    step((1, 2))
    q_wait(2)
    step((3, 4))
    q_copy(0, last_chunk).wait_recv()
    q_copy(1, last_chunk).start()
    step((5, 6), (0, 1))
    q_wait(last_chunk)
    step((7, 8), (2, 3))
    step((9, 10), (4, 5))
    step((11,), (6, 7))
    for w in late:
        w.wait()
    step((12,), (8, 9), (0,))
    step((13,), (10,))
    y_chip(0)
    step((14,), (11,))
    step((15,), (12,))
    attend(n_pair - 1)
    pair_copy((n_pair - 1,)).start()

    def last_merge(p):
        pair_copy((p,)).wait_recv()
        merge_pair(p)
        chip_copy((p,)).start()

    def last_project(g):
        chip_wait(g)
        project(g)
        y_copy(0, g).start()

    last_merge(13)
    last_merge(14)
    last_merge(15)
    last_project(1)
    last_project(2)
    y_chip(1)
    y_final(0)
    last_project(3)
    y_chip(2)
    y_final(1)
    y_chip(3)
    for i in (0, 1):
        last_copy(i).start()
    y_final(2)
    some = f_rcv.at[0:n_group - 1]
    remote(some, some, f_send, f_recv, sib).wait_recv()
    for g in range(n_group - 1):
        put(g, f_src[g].astype(F32), f_rcv[g].astype(F32))
    remote(qall.at[0:3], qall.at[0:3], q_send, q_recv.at[0], sib).wait_send()
    remote(r1, r1, a_send, a_recv.at[0], sib).wait_send()
    remote(r2, r2, c_send, c_recv.at[0], cnt).wait_send()
    remote(some, some, f_send, f_recv, sib).wait_send()
    both = y_src.at[:, 0:2]
    remote(both, both, y_send, y_recv.at[0, 0], sib).wait_send()
    remote(y_last, y_last, l_send, l_recv, sib).wait_send()
    g = n_group - 1
    y_copy(1, g).wait_recv()
    remote(y_last, y_last, l_send, l_recv, sib).wait_recv()
    put(g, hid_half(g, c) + (yc[g] + yr2[g]), hid_half(g, 1 - c) + (y_last[0] + y_last[1]))


def solution(mesh):
    row_spec = P('batch', None)
    cache_spec = P('batch', 'seq', None)
    in_specs = (row_spec, P('batch'), cache_spec, cache_spec, P(None, 'seq', None), P(None, 'seq', None), P('seq', None, None), P('seq', None, None), P('seq', None, None))

    def mla_step(hidden, lengths, c_kv, k_rope, w_uq, w_qr, w_uk, w_uv, w_o):
        n_rows, d_model = hidden.shape
        _, shard, lat = c_kv.shape
        rope = k_rope.shape[2]
        n_head, nope = w_uq.shape[1], w_uq.shape[2]
        n_pair = n_rows // 2
        n_group = n_pair // GROUP
        wide = lat + STAT
        half = d_model // 2
        hid3 = hidden.reshape(n_group, 8, d_model)
        operands = (
            lengths,
            hidden,
            hid3,
            w_uq.reshape(d_model * n_head, nope),
            jnp.transpose(w_qr, (1, 2, 0)).reshape(n_head * rope, d_model),
            w_uk.reshape(n_head * nope, lat),
            w_uv,
            w_o.reshape(n_head * w_o.shape[1], d_model),
            c_kv,
            jnp.transpose(k_rope, (0, 2, 1)),
        )
        operands = tuple(pltpu.with_memory_space_constraint(a, pltpu.HBM) for a in operands)
        vm = pltpu.VMEM
        dma = pltpu.SemaphoreType.DMA
        out = pl.pallas_call(
            kernel,
            out_shape=jax.ShapeDtypeStruct((n_group, 8, d_model), BF16),
            in_specs=[pl.BlockSpec(memory_space=pltpu.HBM)] * len(operands),
            out_specs=pl.BlockSpec(memory_space=pltpu.VMEM),
            scratch_shapes=[
                pltpu.SMEM((n_rows,), jnp.int32),
                vm(hidden.shape, BF16),
                vm(hid3.shape, BF16),
                vm((n_head * n_rows, d_model), BF16),
                vm(operands[3].shape, BF16),
                vm(operands[4].shape, BF16),
                vm(operands[5].shape, BF16),
                vm(operands[6].shape, BF16),
                vm(operands[7].shape, BF16),
                vm(c_kv.shape, BF16),
                vm(operands[9].shape, BF16),
                vm((n_head * n_rows, n_head * d_model), BF16),
                vm((4, n_pair, 8, wide), BF16),
                vm((2, 2, 16, shard), F32),
                vm((2, n_rows, 8, wide), F32),
                vm((n_rows, 8, wide), F32),
                vm((n_pair, 8, wide), F32),
                vm((n_pair, 8, wide), F32),
                vm((n_pair, 8, wide), F32),
                vm((n_group, 2, 8, half), F32),
                vm((n_group, 8, half), F32),
                vm((n_group, 8, half), F32),
                vm((n_group, 8, half), F32),
                vm((n_group, 8, half), BF16),
                vm((n_group, 8, half), BF16),
                vm((2, 8, half), F32),
                dma((8,)),
                dma((5,)),
                dma((5,)),
                dma(()),
                dma((5,)),
                dma(()),
                dma((11,)),
                dma(()),
                dma((n_group,)),
                dma(()),
                dma((2, n_group)),
                dma(()),
                dma(()),
                dma(()),
                dma(()),
            ],
            compiler_params=pltpu.CompilerParams(
                collective_id=0, has_side_effects=True, vmem_limit_bytes=52 * 1024 * 1024,
            ),
            name="mla_decode",
        )(*operands)
        return out.reshape(n_rows, d_model)

    return jax.shard_map(mla_step, mesh=mesh, in_specs=in_specs, out_specs=row_spec, check_vma=False)
```

time: 36.8 us -> 34.6 us (0.940)
  Pallas kernels: 36.1 us -> 33.8 us
    pallas_call x1, Pallas kernels: 36.1 us -> 33.8 us  [mla_step(): pl.pallas_call(kernel, out_shape=jax.ShapeDtypeStruct((n_group, 8, d_mode...]
where the time goes in v4:
time: 34.6 us; the launch traced here: 34.4 us
  Pallas kernels  33.8 us (98%)
  local copies, waits for them, and re-layouts  0.66 us (2%)
    pallas_call x1, Pallas kernels, mla_step(): pl.pallas_call(kernel, out_shape=jax.ShapeDtypeStruct((n_group, 8, d_mode...  33.8 us

profile of v4, /device:TPU:0, one launch (start us, length us, event | category | flops | bytes accessed | tf_op | source)
XLA Modules:
  0.0 34.4 jit_solution(15482258017601162333)
XLA Ops:
  0.0 33.8 %mla_decode.1 = bf16[4,8,2048]{2,1,0:T(8,128)(2,1)S(1)} custom-call(s32[32]{0:T(128)} %len_hbm.1, bf16[32,2048]{1,0:T(8,128)(2,1)} %hid_hbm.1, bf16[4,8,2048]{2,1,0:T(8,128)(2,1)} %bitcast.15, bf16[8192,128]{1,0:T(8,128)(2,1)} %bitcast.11, bf16[256,2048]{1,0:T(8,128)(2,1)} %bitcast.13, bf16[512,512]{1,0:T(8,128)(2,1)} %bitcast.14, ...), custom_call_target="tpu_custom_call" | custom-call | tf_op jit(solution)/shard_map/mla_decode/pallas_call | solution.py:370
  33.8 0.7 %copy.11 = bf16[32,2048]{1,0:T(8,128)(2,1)} copy(bf16[32,2048]{1,0:T(8,128)(2,1)S(1)} %bitcast.9) | data formatting | bytes 262144

commit v5 on v4

--- a/solution.py
+++ b/solution.py
@@ -114,20 +114,24 @@
 
     pl.semaphore_wait(barrier, 3)
 
-    chunks = ((0, 1), (1, 3), (3, 7), (7, n_pair))
-    last_chunk = len(chunks) - 1
+    chunks = ((0, 1), (1, 3), (3, 7), (7, 11), (11, n_pair))
+    n_direct = 3
 
     def q_copy(kind, g):
-        forward = g == last_chunk and kind == 1
+        forward = g >= n_direct and kind == 1
         slot, peer = ((me, cnt), (cnt, sib) if forward else (me, far), (me, sib))[kind]
         rows = qall.at[slot, chunks[g][0]:chunks[g][1]]
-        return remote(rows, rows, q_send, q_recv.at[g + 1 if g == last_chunk and kind == 0 else g], peer)
+        return remote(rows, rows, q_send, q_recv.at[g + 2 if g >= n_direct and kind == 0 else g], peer)
 
     def q_wait(g):
-        rows = qall.at[0:2 if g == last_chunk else 3, chunks[g][0]:chunks[g][1]]
+        rows = qall.at[0:2 if g >= n_direct else 3, chunks[g][0]:chunks[g][1]]
         remote(rows, rows, q_send, q_recv.at[g], sib).wait_recv()
 
-    for g in range(last_chunk):
+    def q_forward(g):
+        q_copy(0, g).wait_recv()
+        q_copy(1, g).start()
+
+    for g in range(n_direct):
         for kind in range(3):
             q_copy(kind, g).start()
 
@@ -166,7 +170,7 @@
                 acc_src[k, b, :, 0:lat] = acc[8 * k:8 * k + 8]
                 acc_src[k, b, :, lat:lat + STAT] = stat[8 * k:8 * k + 8]
 
-    sends = ((0, 1), (2, 3), (4, 5), (6, 7), (8, 9), (10,), (11,), (12,), (13,), (14,), (15,))
+    sends = ((0, 1), (2, 3), (4, 5), (6, 7), (8, 9), (10, 11), (12,), (13,), (14,), (15,))
 
     def pair_copy(ps):
         rows = slice(2 * ps[0], 2 * ps[-1] + 2)
@@ -208,7 +212,7 @@
 
     n_out = 8 * GROUP
 
-    def project(g):
+    def project(g, split=False):
         o_lat = jnp.concatenate([o_rows(GROUP * g + i) for i in range(GROUP)], axis=0).astype(BF16)
         head = iota((n_out, nope), 0) % 4
         wide = []
@@ -219,8 +223,14 @@
         r = iota((8, n_out), 1)
         gather = (iota((8, n_out), 0) == row_of(r)).astype(F32).astype(BF16)
         o_val = dot(gather, wide).astype(BF16)
-        for k in (0, 1):
-            y_src[g, k] = dot(o_val, wo_v[:, k * half_d:(k + 1) * half_d])
+        if not split:
+            for k in (0, 1):
+                y_src[g, k] = dot(o_val, wo_v[:, k * half_d:(k + 1) * half_d])
+            return
+        for k in (1 - c, c):
+            y_src[g, k] = dot(o_val, wo_v[:, pl.ds(pl.multiple_of(k * half_d, half_d), half_d)])
+            if k is not c:
+                y_copy(0, g).start()
 
     def y_copy(kind, g):
         if kind == 0:
@@ -271,54 +281,57 @@
             y_copy(0, g).start()
 
     q_wait(0)
-    for kind in (0, 2):
-        q_copy(kind, last_chunk).start()
+    for g in range(n_direct, len(chunks)):
+        for kind in (0, 2):
+            q_copy(kind, g).start()
     wait_rows(0)
     scores(0)
     q_wait(1)
     step((1, 2))
     q_wait(2)
     step((3, 4))
-    q_copy(0, last_chunk).wait_recv()
-    q_copy(1, last_chunk).start()
+    q_forward(3)
     step((5, 6), (0, 1))
-    q_wait(last_chunk)
+    q_forward(4)
+    q_wait(3)
     step((7, 8), (2, 3))
     step((9, 10), (4, 5))
-    step((11,), (6, 7))
+    q_wait(4)
+    step((11, 12), (6, 7))
     for w in late:
         w.wait()
-    step((12,), (8, 9), (0,))
-    step((13,), (10,))
-    y_chip(0)
-    step((14,), (11,))
+    step((13,), (8, 9))
+    step((14,), (10, 11), (0,))
     step((15,), (12,))
     attend(n_pair - 1)
     pair_copy((n_pair - 1,)).start()
 
-    def last_merge(p):
-        pair_copy((p,)).wait_recv()
-        merge_pair(p)
-        chip_copy((p,)).start()
+    def last_merge(ps):
+        pair_copy(ps).wait_recv()
+        for p in ps:
+            merge_pair(p)
+        chip_copy(ps).start()
 
     def last_project(g):
         chip_wait(g)
-        project(g)
-        y_copy(0, g).start()
-
-    last_merge(13)
-    last_merge(14)
-    last_merge(15)
+        project(g, g == n_group - 1)
+        if g < n_group - 1:
+            y_copy(0, g).start()
+
+    last_merge((13,))
+    last_merge((14,))
+    last_merge((15,))
     last_project(1)
+    y_chip(0)
     last_project(2)
     y_chip(1)
     y_final(0)
+    y_chip(2)
     last_project(3)
-    y_chip(2)
-    y_final(1)
     y_chip(3)
     for i in (0, 1):
         last_copy(i).start()
+    y_final(1)
     y_final(2)
     some = f_rcv.at[0:n_group - 1]
     remote(some, some, f_send, f_recv, sib).wait_recv()
@@ -403,9 +416,9 @@
                 dma((5,)),
                 dma((5,)),
                 dma(()),
-                dma((5,)),
-                dma(()),
-                dma((11,)),
+                dma((7,)),
+                dma(()),
+                dma((10,)),
                 dma(()),
                 dma((n_group,)),
                 dma(()),
@@ -416,7 +429,7 @@
                 dma(()),
             ],
             compiler_params=pltpu.CompilerParams(
-                collective_id=0, has_side_effects=True, vmem_limit_bytes=52 * 1024 * 1024,
+                collective_id=0, has_side_effects=True, vmem_limit_bytes=53 * 1024 * 1024,
             ),
             name="mla_decode",
         )(*operands)

time: 34.6 us -> 35.3 us (1.020)
  Pallas kernels: 33.8 us -> 34.5 us
    pallas_call x1, Pallas kernels: 33.8 us -> 34.5 us  [mla_step(): pl.pallas_call(kernel, out_shape=jax.ShapeDtypeStruct((n_group, 8, d_mode...]
where the time goes in v5:
time: 35.3 us; the launch traced here: 35.2 us
  Pallas kernels  34.5 us (98%)
  local copies, waits for them, and re-layouts  0.66 us (2%)
    pallas_call x1, Pallas kernels, mla_step(): pl.pallas_call(kernel, out_shape=jax.ShapeDtypeStruct((n_group, 8, d_mode...  34.5 us

profile of v5, /device:TPU:0, one launch (start us, length us, event | category | flops | bytes accessed | tf_op | source)
XLA Modules:
  0.0 35.2 jit_solution(313212662999867073)
XLA Ops:
  0.0 34.5 %mla_decode.1 = bf16[4,8,2048]{2,1,0:T(8,128)(2,1)S(1)} custom-call(s32[32]{0:T(128)} %len_hbm.1, bf16[32,2048]{1,0:T(8,128)(2,1)} %hid_hbm.1, bf16[4,8,2048]{2,1,0:T(8,128)(2,1)} %bitcast.15, bf16[8192,128]{1,0:T(8,128)(2,1)} %bitcast.11, bf16[256,2048]{1,0:T(8,128)(2,1)} %bitcast.13, bf16[512,512]{1,0:T(8,128)(2,1)} %bitcast.14, ...), custom_call_target="tpu_custom_call" | custom-call | tf_op jit(solution)/shard_map/mla_decode/pallas_call | solution.py:383
  34.5 0.7 %copy.11 = bf16[32,2048]{1,0:T(8,128)(2,1)} copy(bf16[32,2048]{1,0:T(8,128)(2,1)S(1)} %bitcast.9) | data formatting | bytes 262144

commit v6 on v5

--- a/solution.py
+++ b/solution.py
@@ -30,7 +30,7 @@
     len_hbm, hid_hbm, hid3_hbm, wuq_hbm, wqr_hbm, wuk_hbm, wuv_hbm, wo_hbm, ckv_hbm, kr_hbm,
     out_ref,
     len_s, hid_v, hid3_v, hid_r, wuq_v, wqr_v, wuk_v, wuv_v, wo_v, ckv_v, kr_v,
-    em_v, qall, sbuf, acc_src, r1, s2, keep_v, r2, y_src, yr1, yc, yr2, f_src, f_rcv, y_last,
+    em_v, qall, sbuf, acc_src, r1, s2, keep_v, r2, y_src, yr1, yc, yr2, f_src, f_rcv, l_src, l_r1, l_sum, l_all,
     w_sem, ckv_sem, kr_sem, q_send, q_recv, a_send, a_recv, c_send, c_recv, y_send, y_recv, f_send, f_recv, l_send, l_recv,
 ):
     n_rows = ckv_hbm.shape[0]
@@ -39,7 +39,6 @@
     rope = kr_hbm.shape[1]
     nope = wuq_hbm.shape[1]
     n_pair = n_rows // 2
-    n_group = n_pair // GROUP
     d_model = hid_hbm.shape[1]
     half_d = d_model // 2
     scale = 1.0 / math.sqrt(nope + rope)
@@ -170,6 +169,8 @@
                 acc_src[k, b, :, 0:lat] = acc[8 * k:8 * k + 8]
                 acc_src[k, b, :, lat:lat + STAT] = stat[8 * k:8 * k + 8]
 
+    groups = ((0, 4), (4, 8), (8, 12), (12, 14), (14, n_pair))
+    n_full = 3
     sends = ((0, 1), (2, 3), (4, 5), (6, 7), (8, 9), (10, 11), (12,), (13,), (14,), (15,))
 
     def pair_copy(ps):
@@ -178,10 +179,11 @@
 
     def chip_copy(ps):
         rows = slice(ps[0], ps[-1] + 1)
-        return remote(s2.at[rows], r2.at[rows], c_send, c_recv.at[ps[0] // GROUP], cnt)
+        g = max(i for i, group in enumerate(groups) if group[0] <= ps[0])
+        return remote(s2.at[rows], r2.at[rows], c_send, c_recv.at[g], cnt)
 
     def chip_wait(g):
-        rows = r2.at[GROUP * g:GROUP * (g + 1)]
+        rows = r2.at[groups[g][0]:groups[g][1]]
         remote(rows, rows, c_send, c_recv.at[g], cnt).wait_recv()
 
     def merge(a, b):
@@ -210,27 +212,33 @@
         acc, _, l = merge(keep_v[p], r2[p])
         return acc / l
 
-    n_out = 8 * GROUP
-
-    def project(g, split=False):
-        o_lat = jnp.concatenate([o_rows(GROUP * g + i) for i in range(GROUP)], axis=0).astype(BF16)
+    def project(first, last):
+        n_out, n_b = 8 * (last - first), 2 * (last - first)
+        o_lat = jnp.concatenate([o_rows(p) for p in range(first, last)], axis=0).astype(BF16)
         head = iota((n_out, nope), 0) % 4
         wide = []
         for h in range(0, n_head, 2):
             two = dot(o_lat, jnp.concatenate([wuv_v[h], wuv_v[h + 1]], axis=1))
             wide += [jnp.where(head == h + i, two[:, i * nope:(i + 1) * nope], 0.0).astype(BF16) for i in (0, 1)]
         wide = jnp.concatenate(wide, axis=1)
-        r = iota((8, n_out), 1)
-        gather = (iota((8, n_out), 0) == row_of(r)).astype(F32).astype(BF16)
+        r = iota((n_b, n_out), 1)
+        gather = (iota((n_b, n_out), 0) == row_of(r)).astype(F32).astype(BF16)
         o_val = dot(gather, wide).astype(BF16)
-        if not split:
-            for k in (0, 1):
-                y_src[g, k] = dot(o_val, wo_v[:, k * half_d:(k + 1) * half_d])
-            return
-        for k in (1 - c, c):
-            y_src[g, k] = dot(o_val, wo_v[:, pl.ds(pl.multiple_of(k * half_d, half_d), half_d)])
-            if k is not c:
-                y_copy(0, g).start()
+        return lambda k: dot(o_val, wo_v[:, pl.ds(pl.multiple_of(k * half_d, half_d), half_d)])
+
+    def project_full(g, n=1):
+        y = project(groups[g][0], groups[g + n - 1][1])
+        for k in (0, 1):
+            part = y(k)
+            for i in range(n):
+                y_src[g + i, k] = part[8 * i:8 * i + 8]
+
+    def project_last(g):
+        y = project(*groups[g])
+        i = g - n_full
+        l_src[i, 1 - c] = y(1 - c)
+        remote(l_src.at[i, 1 - c], l_r1.at[i], l_send.at[0], l_recv.at[0, i], sib).start()
+        l_src[i, c] = y(c)
 
     def y_copy(kind, g):
         if kind == 0:
@@ -240,44 +248,55 @@
     def f_copy(g):
         return remote(f_src.at[g], f_rcv.at[g], f_send, f_recv, sib)
 
-    def last_copy(i):
-        return remote(yc.at[n_group - 1], y_last.at[i], l_send, l_recv, (sib, far)[i])
+    def last_chip(g):
+        i = g - n_full
+        remote(l_r1.at[i], l_r1.at[i], l_send.at[0], l_recv.at[0, i], sib).wait_recv()
+        l_sum[i] = l_src[i, c] + l_r1[i]
+        for k, peer in enumerate((cnt, far, sib)):
+            remote(l_sum.at[i], l_all.at[i, k], l_send.at[1], l_recv.at[1, i], peer).start()
+
+    def last_final(g):
+        i = g - n_full
+        remote(l_all.at[i], l_all.at[i], l_send.at[1], l_recv.at[1, i], sib).wait_recv()
+        rows = slice(2 * groups[g][0] % 8, (2 * groups[g][1] - 1) % 8 + 1)
+        put(2 * groups[g][0] // 8, rows, l_sum[i] + l_all[i, 0], l_all[i, 2] + l_all[i, 1])
 
     def y_chip(g):
         y_copy(0, g).wait_recv()
         yc[g] = y_src[g, c] + yr1[g]
         y_copy(1, g).start()
 
-    def hid_half(g, k):
-        return hid3_v[g, :, pl.ds(pl.multiple_of(k * half_d, half_d), half_d)].astype(F32)
+    def hid_half(g, k, rows=slice(None)):
+        return hid3_v[g, rows, pl.ds(pl.multiple_of(k * half_d, half_d), half_d)].astype(F32)
 
     def y_final(g):
         y_copy(1, g).wait_recv()
         f_src[g] = (hid_half(g, c) + (yc[g] + yr2[g])).astype(BF16)
         f_copy(g).start()
 
-    def put(g, mine, other):
-        out_ref[g, :, 0:half_d] = jnp.where(c == 0, mine, other).astype(BF16)
-        out_ref[g, :, half_d:d_model] = jnp.where(c == 0, other, mine).astype(BF16)
-
-    def step(js, merges=(), groups=()):
+    def put(g, rows, mine, other):
+        hid = hid3_v[g, rows, :].astype(F32)
+        out_ref[g, rows, 0:half_d] = (hid[:, :half_d] + jnp.where(c == 0, mine, other)).astype(BF16)
+        out_ref[g, rows, half_d:d_model] = (hid[:, half_d:] + jnp.where(c == 0, other, mine)).astype(BF16)
+
+    def step(js, merges=(), ready=()):
         for j in js:
             wait_rows(j)
         if merges:
             pair_copy(merges).wait_recv()
-        for g in groups:
+        for g in ready:
             chip_wait(g)
         for j in js:
             scores(j)
             attend(j - 1)
         for p in merges:
             merge_pair(p)
-        for g in groups:
-            project(g)
+        for g in ready:
+            project_full(g)
         pair_copy(tuple(j - 1 for j in js)).start()
         if merges:
             chip_copy(merges).start()
-        for g in groups:
+        for g in ready:
             y_copy(0, g).start()
 
     q_wait(0)
@@ -312,42 +331,39 @@
             merge_pair(p)
         chip_copy(ps).start()
 
-    def last_project(g):
-        chip_wait(g)
-        project(g, g == n_group - 1)
-        if g < n_group - 1:
-            y_copy(0, g).start()
-
     last_merge((13,))
     last_merge((14,))
     last_merge((15,))
-    last_project(1)
     y_chip(0)
-    last_project(2)
+    chip_wait(1)
+    chip_wait(2)
+    project_full(1, 2)
+    for g in (1, 2):
+        y_copy(0, g).start()
     y_chip(1)
-    y_final(0)
     y_chip(2)
-    last_project(3)
-    y_chip(3)
-    for i in (0, 1):
-        last_copy(i).start()
-    y_final(1)
-    y_final(2)
-    some = f_rcv.at[0:n_group - 1]
-    remote(some, some, f_send, f_recv, sib).wait_recv()
-    for g in range(n_group - 1):
-        put(g, f_src[g].astype(F32), f_rcv[g].astype(F32))
+    chip_wait(3)
+    project_last(3)
+    chip_wait(4)
+    project_last(4)
+    last_chip(3)
+    last_chip(4)
+    for g in range(n_full):
+        y_final(g)
+    remote(f_rcv, f_rcv, f_send, f_recv, sib).wait_recv()
+    for g in range(n_full):
+        mine, other = f_src[g].astype(F32), f_rcv[g].astype(F32)
+        out_ref[g, :, 0:half_d] = jnp.where(c == 0, mine, other).astype(BF16)
+        out_ref[g, :, half_d:d_model] = jnp.where(c == 0, other, mine).astype(BF16)
+    last_final(3)
     remote(qall.at[0:3], qall.at[0:3], q_send, q_recv.at[0], sib).wait_send()
     remote(r1, r1, a_send, a_recv.at[0], sib).wait_send()
     remote(r2, r2, c_send, c_recv.at[0], cnt).wait_send()
-    remote(some, some, f_send, f_recv, sib).wait_send()
-    both = y_src.at[:, 0:2]
-    remote(both, both, y_send, y_recv.at[0, 0], sib).wait_send()
-    remote(y_last, y_last, l_send, l_recv, sib).wait_send()
-    g = n_group - 1
-    y_copy(1, g).wait_recv()
-    remote(y_last, y_last, l_send, l_recv, sib).wait_recv()
-    put(g, hid_half(g, c) + (yc[g] + yr2[g]), hid_half(g, 1 - c) + (y_last[0] + y_last[1]))
+    remote(f_rcv, f_rcv, f_send, f_recv, sib).wait_send()
+    remote(y_src, y_src, y_send, y_recv.at[0, 0], sib).wait_send()
+    remote(l_r1, l_r1, l_send.at[0], l_recv.at[0, 0], sib).wait_send()
+    remote(l_all, l_all, l_send.at[1], l_recv.at[0, 0], sib).wait_send()
+    last_final(4)
 
 
 def solution(mesh):
@@ -405,13 +421,16 @@
                 vm((n_pair, 8, wide), F32),
                 vm((n_pair, 8, wide), F32),
                 vm((n_pair, 8, wide), F32),
-                vm((n_group, 2, 8, half), F32),
-                vm((n_group, 8, half), F32),
-                vm((n_group, 8, half), F32),
-                vm((n_group, 8, half), F32),
-                vm((n_group, 8, half), BF16),
-                vm((n_group, 8, half), BF16),
-                vm((2, 8, half), F32),
+                vm((3, 2, 8, half), F32),
+                vm((3, 8, half), F32),
+                vm((3, 8, half), F32),
+                vm((3, 8, half), F32),
+                vm((3, 8, half), BF16),
+                vm((3, 8, half), BF16),
+                vm((2, 2, 4, half), F32),
+                vm((2, 4, half), F32),
+                vm((2, 4, half), F32),
+                vm((2, 3, 4, half), F32),
                 dma((8,)),
                 dma((5,)),
                 dma((5,)),
@@ -420,13 +439,13 @@
                 dma(()),
                 dma((10,)),
                 dma(()),
-                dma((n_group,)),
-                dma(()),
-                dma((2, n_group)),
-                dma(()),
-                dma(()),
-                dma(()),
-                dma(()),
+                dma((5,)),
+                dma(()),
+                dma((2, 3)),
+                dma(()),
+                dma(()),
+                dma((2,)),
+                dma((2, 2)),
             ],
             compiler_params=pltpu.CompilerParams(
                 collective_id=0, has_side_effects=True, vmem_limit_bytes=53 * 1024 * 1024,

time: 35.3 us -> 34.2 us (0.969)
  Pallas kernels: 34.5 us -> 33.4 us
    pallas_call x1, Pallas kernels: 34.5 us -> 33.4 us  [mla_step(): pl.pallas_call(kernel, out_shape=jax.ShapeDtypeStruct((n_group, 8, d_mode...]
where the time goes in v6:
time: 34.2 us; the launch traced here: 34.1 us
  Pallas kernels  33.4 us (98%)
  local copies, waits for them, and re-layouts  0.66 us (2%)
    pallas_call x1, Pallas kernels, mla_step(): pl.pallas_call(kernel, out_shape=jax.ShapeDtypeStruct((n_group, 8, d_mode...  33.4 us

profile of v6, /device:TPU:0, one launch (start us, length us, event | category | flops | bytes accessed | tf_op | source)
XLA Modules:
  0.0 34.1 jit_solution(5879605152469285940)
XLA Ops:
  0.0 33.4 %mla_decode.1 = bf16[4,8,2048]{2,1,0:T(8,128)(2,1)S(1)} custom-call(s32[32]{0:T(128)} %len_hbm.1, bf16[32,2048]{1,0:T(8,128)(2,1)} %hid_hbm.1, bf16[4,8,2048]{2,1,0:T(8,128)(2,1)} %bitcast.15, bf16[8192,128]{1,0:T(8,128)(2,1)} %bitcast.11, bf16[256,2048]{1,0:T(8,128)(2,1)} %bitcast.13, bf16[512,512]{1,0:T(8,128)(2,1)} %bitcast.14, ...), custom_call_target="tpu_custom_call" | custom-call | tf_op jit(solution)/shard_map/mla_decode/pallas_call | solution.py:399
  33.4 0.7 %copy.11 = bf16[32,2048]{1,0:T(8,128)(2,1)} copy(bf16[32,2048]{1,0:T(8,128)(2,1)S(1)} %bitcast.9) | data formatting | bytes 262144

commit v7 on v6

--- a/solution.py
+++ b/solution.py
@@ -30,8 +30,8 @@
     len_hbm, hid_hbm, hid3_hbm, wuq_hbm, wqr_hbm, wuk_hbm, wuv_hbm, wo_hbm, ckv_hbm, kr_hbm,
     out_ref,
     len_s, hid_v, hid3_v, hid_r, wuq_v, wqr_v, wuk_v, wuv_v, wo_v, ckv_v, kr_v,
-    em_v, qall, sbuf, acc_src, r1, s2, keep_v, r2, y_src, yr1, yc, yr2, f_src, f_rcv, l_src, l_r1, l_sum, l_all,
-    w_sem, ckv_sem, kr_sem, q_send, q_recv, a_send, a_recv, c_send, c_recv, y_send, y_recv, f_send, f_recv, l_send, l_recv,
+    em_v, qall, sbuf, acc_src, r1, s2, keep_v, r2, y_src, yr1, yc, yr2, f_src, f_rcv, h_src, h_rcv, l_src, l_r1, l_sum, l_all,
+    w_sem, ckv_sem, sent, q_recv, a_recv, c_recv, y_recv, f_recv, h_recv, l_recv,
 ):
     n_rows = ckv_hbm.shape[0]
     shard = ckv_hbm.shape[1]
@@ -54,14 +54,14 @@
         return pltpu.make_async_copy(src, dst, sem)
 
     hid_load = load(hid_hbm, hid_v, w_sem.at[0])
-    early = [load(src, dst, w_sem.at[1 + i]) for i, (src, dst) in enumerate((
-        (wqr_hbm, wqr_v), (wuk_hbm, wuk_v), (len_hbm, len_s), (hid3_hbm, hid3_v), (wuq_hbm, wuq_v)))]
-    late = [load(src, dst, w_sem.at[6 + i]) for i, (src, dst) in enumerate(((wuv_hbm, wuv_v), (wo_hbm, wo_v)))]
+    early = [load(src, dst, w_sem.at[min(1 + i, 3)]) for i, (src, dst) in enumerate((
+        (wqr_hbm, wqr_v), (wuq_hbm, wuq_v), (wuk_hbm, wuk_v), (len_hbm, len_s), (hid3_hbm, hid3_v)))]
+    late = [load(src, dst, w_sem.at[4]) for src, dst in ((wuv_hbm, wuv_v), (wo_hbm, wo_v))]
     spans = ((0, 1), (1, 3), (3, 7), (7, 11), (11, n_pair))
 
     def row_loads(i):
         rows = slice(2 * spans[i][0], 2 * spans[i][1])
-        return (load(kr_hbm.at[rows], kr_v.at[rows], kr_sem.at[i]), load(ckv_hbm.at[rows], ckv_v.at[rows], ckv_sem.at[i]))
+        return (load(kr_hbm.at[rows], kr_v.at[rows], ckv_sem.at[i]), load(ckv_hbm.at[rows], ckv_v.at[rows], ckv_sem.at[i]))
 
     for w in (hid_load, *early):
         w.start()
@@ -99,13 +99,15 @@
     for k in range(d_model // nope):
         wide = dot(hid_r[:, k * nope:(k + 1) * nope], spread)
         em_v[:, k * n_head * nope:(k + 1) * n_head * nope] = jnp.where(same_head, wide, 0.0).astype(BF16)
-    for w in early:
+    for w in early[:2]:
         w.wait()
     q_r = dot_t(hid_r[...], wqr_v[...])
     q_n = dot(em_v[...], wuq_v[...])
     q_r = jnp.where(iota((n_local, n_head * rope), 1) // rope == iota((n_local, n_head * rope), 0) % 4, q_r, 0.0)
     q_r = dot(q_r.astype(BF16), fold).astype(BF16)
     q_wide = jnp.concatenate([jnp.where(r_h == h, q_n, 0.0).astype(BF16) for h in range(n_head)], axis=1)
+    for w in early[2:]:
+        w.wait()
     q_l = dot(q_wide, wuk_v[...]).astype(BF16)
     for p in range(n_pair):
         qall[me, p, :, 0:lat] = q_l[8 * p:8 * p + 8]
@@ -120,11 +122,11 @@
         forward = g >= n_direct and kind == 1
         slot, peer = ((me, cnt), (cnt, sib) if forward else (me, far), (me, sib))[kind]
         rows = qall.at[slot, chunks[g][0]:chunks[g][1]]
-        return remote(rows, rows, q_send, q_recv.at[g + 2 if g >= n_direct and kind == 0 else g], peer)
+        return remote(rows, rows, sent, q_recv.at[g + 2 if g >= n_direct and kind == 0 else g], peer)
 
     def q_wait(g):
         rows = qall.at[0:2 if g >= n_direct else 3, chunks[g][0]:chunks[g][1]]
-        remote(rows, rows, q_send, q_recv.at[g], sib).wait_recv()
+        remote(rows, rows, sent, q_recv.at[g], sib).wait_recv()
 
     def q_forward(g):
         q_copy(0, g).wait_recv()
@@ -175,16 +177,16 @@
 
     def pair_copy(ps):
         rows = slice(2 * ps[0], 2 * ps[-1] + 2)
-        return remote(acc_src.at[1 - c, rows], r1.at[rows], a_send, a_recv.at[sends.index(ps)], sib)
+        return remote(acc_src.at[1 - c, rows], r1.at[rows], sent, a_recv.at[sends.index(ps)], sib)
 
     def chip_copy(ps):
         rows = slice(ps[0], ps[-1] + 1)
         g = max(i for i, group in enumerate(groups) if group[0] <= ps[0])
-        return remote(s2.at[rows], r2.at[rows], c_send, c_recv.at[g], cnt)
+        return remote(s2.at[rows], r2.at[rows], sent, c_recv.at[g], cnt)
 
     def chip_wait(g):
         rows = r2.at[groups[g][0]:groups[g][1]]
-        remote(rows, rows, c_send, c_recv.at[g], cnt).wait_recv()
+        remote(rows, rows, sent, c_recv.at[g], cnt).wait_recv()
 
     def merge(a, b):
         m1, l1 = a[:, lat:lat + 1], a[:, lat + STAT // 2:lat + STAT // 2 + 1]
@@ -226,40 +228,54 @@
         o_val = dot(gather, wide).astype(BF16)
         return lambda k: dot(o_val, wo_v[:, pl.ds(pl.multiple_of(k * half_d, half_d), half_d)])
 
-    def project_full(g, n=1):
-        y = project(groups[g][0], groups[g + n - 1][1])
+    def project_full(g):
+        y = project(*groups[g])
         for k in (0, 1):
-            part = y(k)
-            for i in range(n):
-                y_src[g + i, k] = part[8 * i:8 * i + 8]
+            y_src[g, k] = y(k)
 
     def project_last(g):
         y = project(*groups[g])
         i = g - n_full
         l_src[i, 1 - c] = y(1 - c)
-        remote(l_src.at[i, 1 - c], l_r1.at[i], l_send.at[0], l_recv.at[0, i], sib).start()
+        remote(l_src.at[i, 1 - c], l_r1.at[i], sent, l_recv.at[0, i], sib).start()
         l_src[i, c] = y(c)
 
     def y_copy(kind, g):
         if kind == 0:
-            return remote(y_src.at[g, 1 - c], yr1.at[g], y_send, y_recv.at[0, g], sib)
-        return remote(yc.at[g], yr2.at[g], y_send, y_recv.at[1, g], cnt)
+            return remote(y_src.at[g, 1 - c], yr1.at[g], sent, y_recv.at[0, g], sib)
+        return remote(yc.at[g], yr2.at[g], sent, y_recv.at[1, g], cnt)
 
     def f_copy(g):
-        return remote(f_src.at[g], f_rcv.at[g], f_send, f_recv, sib)
+        return remote(f_src.at[g], f_rcv.at[g], sent, f_recv, sib)
 
     def last_chip(g):
         i = g - n_full
-        remote(l_r1.at[i], l_r1.at[i], l_send.at[0], l_recv.at[0, i], sib).wait_recv()
+        remote(l_r1.at[i], l_r1.at[i], sent, l_recv.at[0, i], sib).wait_recv()
         l_sum[i] = l_src[i, c] + l_r1[i]
-        for k, peer in enumerate((cnt, far, sib)):
-            remote(l_sum.at[i], l_all.at[i, k], l_send.at[1], l_recv.at[1, i], peer).start()
+        for k, peer in enumerate((cnt, far, sib)[:1 + 2 * i]):
+            remote(l_sum.at[i], l_all.at[i, k], sent, l_recv.at[1, i], peer).start()
+
+    def rows_of(g):
+        return slice(2 * groups[g][0] % 8, (2 * groups[g][1] - 1) % 8 + 1)
+
+    def half_copy():
+        return remote(h_src, h_rcv, sent, h_recv, sib)
+
+    def half_final(g):
+        i = g - n_full
+        remote(l_all.at[i, 0], l_all.at[i, 0], sent, l_recv.at[1, i], sib).wait_recv()
+        h_src[...] = (hid_half(2 * groups[g][0] // 8, c, rows_of(g)) + (l_sum[i] + l_all[i, 0])).astype(BF16)
+        half_copy().start()
 
     def last_final(g):
         i = g - n_full
-        remote(l_all.at[i], l_all.at[i], l_send.at[1], l_recv.at[1, i], sib).wait_recv()
-        rows = slice(2 * groups[g][0] % 8, (2 * groups[g][1] - 1) % 8 + 1)
-        put(2 * groups[g][0] // 8, rows, l_sum[i] + l_all[i, 0], l_all[i, 2] + l_all[i, 1])
+        remote(l_all.at[i], l_all.at[i], sent, l_recv.at[1, i], sib).wait_recv()
+        put(2 * groups[g][0] // 8, rows_of(g), l_sum[i] + l_all[i, 0], l_all[i, 2] + l_all[i, 1])
+
+    def join(g, rows, mine, other):
+        mine, other = mine.astype(F32), other.astype(F32)
+        out_ref[g, rows, 0:half_d] = jnp.where(c == 0, mine, other).astype(BF16)
+        out_ref[g, rows, half_d:d_model] = jnp.where(c == 0, other, mine).astype(BF16)
 
     def y_chip(g):
         y_copy(0, g).wait_recv()
@@ -319,8 +335,8 @@
     step((11, 12), (6, 7))
     for w in late:
         w.wait()
-    step((13,), (8, 9))
-    step((14,), (10, 11), (0,))
+    step((13,), (8, 9), (0,))
+    step((14,), (10, 11))
     step((15,), (12,))
     attend(n_pair - 1)
     pair_copy((n_pair - 1,)).start()
@@ -334,35 +350,35 @@
     last_merge((13,))
     last_merge((14,))
     last_merge((15,))
+    for g in (1, 2):
+        chip_wait(g)
+        project_full(g)
+        y_copy(0, g).start()
     y_chip(0)
-    chip_wait(1)
-    chip_wait(2)
-    project_full(1, 2)
-    for g in (1, 2):
-        y_copy(0, g).start()
     y_chip(1)
-    y_chip(2)
     chip_wait(3)
     project_last(3)
+    y_chip(2)
     chip_wait(4)
     project_last(4)
     last_chip(3)
     last_chip(4)
     for g in range(n_full):
         y_final(g)
-    remote(f_rcv, f_rcv, f_send, f_recv, sib).wait_recv()
+    half_final(3)
+    remote(f_rcv, f_rcv, sent, f_recv, sib).wait_recv()
     for g in range(n_full):
-        mine, other = f_src[g].astype(F32), f_rcv[g].astype(F32)
-        out_ref[g, :, 0:half_d] = jnp.where(c == 0, mine, other).astype(BF16)
-        out_ref[g, :, half_d:d_model] = jnp.where(c == 0, other, mine).astype(BF16)
-    last_final(3)
-    remote(qall.at[0:3], qall.at[0:3], q_send, q_recv.at[0], sib).wait_send()
-    remote(r1, r1, a_send, a_recv.at[0], sib).wait_send()
-    remote(r2, r2, c_send, c_recv.at[0], cnt).wait_send()
-    remote(f_rcv, f_rcv, f_send, f_recv, sib).wait_send()
-    remote(y_src, y_src, y_send, y_recv.at[0, 0], sib).wait_send()
-    remote(l_r1, l_r1, l_send.at[0], l_recv.at[0, 0], sib).wait_send()
-    remote(l_all, l_all, l_send.at[1], l_recv.at[0, 0], sib).wait_send()
+        join(g, slice(None), f_src[g], f_rcv[g])
+    half_copy().wait_recv()
+    join(2 * groups[3][0] // 8, rows_of(3), h_src[...], h_rcv[...])
+    half_copy().wait_send()
+    remote(qall.at[0:3], qall.at[0:3], sent, q_recv.at[0], sib).wait_send()
+    remote(r1, r1, sent, a_recv.at[0], sib).wait_send()
+    remote(r2, r2, sent, c_recv.at[0], cnt).wait_send()
+    remote(f_rcv, f_rcv, sent, f_recv, sib).wait_send()
+    remote(y_src, y_src, sent, y_recv.at[0, 0], sib).wait_send()
+    remote(l_r1, l_r1, sent, l_recv.at[0, 0], sib).wait_send()
+    remote(l_src, l_src, sent, l_recv.at[0, 0], sib).wait_send()
     last_final(4)
 
 
@@ -427,24 +443,21 @@
                 vm((3, 8, half), F32),
                 vm((3, 8, half), BF16),
                 vm((3, 8, half), BF16),
+                vm((4, half), BF16),
+                vm((4, half), BF16),
                 vm((2, 2, 4, half), F32),
                 vm((2, 4, half), F32),
                 vm((2, 4, half), F32),
                 vm((2, 3, 4, half), F32),
-                dma((8,)),
                 dma((5,)),
                 dma((5,)),
                 dma(()),
                 dma((7,)),
-                dma(()),
                 dma((10,)),
-                dma(()),
                 dma((5,)),
-                dma(()),
                 dma((2, 3)),
                 dma(()),
                 dma(()),
-                dma((2,)),
                 dma((2, 2)),
             ],
             compiler_params=pltpu.CompilerParams(

time: 34.2 us -> 33.8 us (0.988)
  Pallas kernels: 33.4 us -> 33 us
    pallas_call x1, Pallas kernels: 33.4 us -> 33 us  [mla_step(): pl.pallas_call(kernel, out_shape=jax.ShapeDtypeStruct((n_group, 8, d_mode...]
where the time goes in v7:
time: 33.8 us; the launch traced here: 33.7 us
  Pallas kernels  33 us (98%)
  local copies, waits for them, and re-layouts  0.66 us (2%)
    pallas_call x1, Pallas kernels, mla_step(): pl.pallas_call(kernel, out_shape=jax.ShapeDtypeStruct((n_group, 8, d_mode...  33 us

profile of v7, /device:TPU:0, one launch (start us, length us, event | category | flops | bytes accessed | tf_op | source)
XLA Modules:
  0.0 33.7 jit_solution(16743126108295698624)
XLA Ops:
  0.0 33.0 %mla_decode.1 = bf16[4,8,2048]{2,1,0:T(8,128)(2,1)S(1)} custom-call(s32[32]{0:T(128)} %len_hbm.1, bf16[32,2048]{1,0:T(8,128)(2,1)} %hid_hbm.1, bf16[4,8,2048]{2,1,0:T(8,128)(2,1)} %bitcast.15, bf16[8192,128]{1,0:T(8,128)(2,1)} %bitcast.11, bf16[256,2048]{1,0:T(8,128)(2,1)} %bitcast.13, bf16[512,512]{1,0:T(8,128)(2,1)} %bitcast.14, ...), custom_call_target="tpu_custom_call" | custom-call | tf_op jit(solution)/shard_map/mla_decode/pallas_call | solution.py:415
  33.0 0.7 %copy.11 = bf16[32,2048]{1,0:T(8,128)(2,1)} copy(bf16[32,2048]{1,0:T(8,128)(2,1)S(1)} %bitcast.9) | data formatting | bytes 262144

commit v8 on v7

--- a/solution.py
+++ b/solution.py
@@ -31,7 +31,7 @@
     out_ref,
     len_s, hid_v, hid3_v, hid_r, wuq_v, wqr_v, wuk_v, wuv_v, wo_v, ckv_v, kr_v,
     em_v, qall, sbuf, acc_src, r1, s2, keep_v, r2, y_src, yr1, yc, yr2, f_src, f_rcv, h_src, h_rcv, l_src, l_r1, l_sum, l_all,
-    w_sem, ckv_sem, sent, q_recv, a_recv, c_recv, y_recv, f_recv, h_recv, l_recv,
+    w_sem, ckv_sem, sent, q_recv, a_recv, c_recv,
 ):
     n_rows = ckv_hbm.shape[0]
     shard = ckv_hbm.shape[1]
@@ -136,6 +136,7 @@
         for kind in range(3):
             q_copy(kind, g).start()
 
+
     upper8 = iota((8, lat + STAT), 0) < 4
 
     def scores(p):
@@ -237,39 +238,39 @@
         y = project(*groups[g])
         i = g - n_full
         l_src[i, 1 - c] = y(1 - c)
-        remote(l_src.at[i, 1 - c], l_r1.at[i], sent, l_recv.at[0, i], sib).start()
+        remote(l_src.at[i, 1 - c], l_r1.at[i], sent, a_recv.at[i], sib).start()
         l_src[i, c] = y(c)
 
     def y_copy(kind, g):
         if kind == 0:
-            return remote(y_src.at[g, 1 - c], yr1.at[g], sent, y_recv.at[0, g], sib)
-        return remote(yc.at[g], yr2.at[g], sent, y_recv.at[1, g], cnt)
+            return remote(y_src.at[g, 1 - c], yr1.at[g], sent, q_recv.at[g], sib)
+        return remote(yc.at[g], yr2.at[g], sent, q_recv.at[(3, 5, 6)[g]], cnt)
 
     def f_copy(g):
-        return remote(f_src.at[g], f_rcv.at[g], sent, f_recv, sib)
+        return remote(f_src.at[g], f_rcv.at[g], sent, a_recv.at[2], sib)
 
     def last_chip(g):
         i = g - n_full
-        remote(l_r1.at[i], l_r1.at[i], sent, l_recv.at[0, i], sib).wait_recv()
+        remote(l_r1.at[i], l_r1.at[i], sent, a_recv.at[i], sib).wait_recv()
         l_sum[i] = l_src[i, c] + l_r1[i]
         for k, peer in enumerate((cnt, far, sib)[:1 + 2 * i]):
-            remote(l_sum.at[i], l_all.at[i, k], sent, l_recv.at[1, i], peer).start()
+            remote(l_sum.at[i], l_all.at[i, k], sent, (q_recv.at[4], c_recv.at[0])[i], peer).start()
 
     def rows_of(g):
         return slice(2 * groups[g][0] % 8, (2 * groups[g][1] - 1) % 8 + 1)
 
     def half_copy():
-        return remote(h_src, h_rcv, sent, h_recv, sib)
+        return remote(h_src, h_rcv, sent, a_recv.at[3], sib)
 
     def half_final(g):
         i = g - n_full
-        remote(l_all.at[i, 0], l_all.at[i, 0], sent, l_recv.at[1, i], sib).wait_recv()
+        remote(l_all.at[i, 0], l_all.at[i, 0], sent, (q_recv.at[4], c_recv.at[0])[i], sib).wait_recv()
         h_src[...] = (hid_half(2 * groups[g][0] // 8, c, rows_of(g)) + (l_sum[i] + l_all[i, 0])).astype(BF16)
         half_copy().start()
 
     def last_final(g):
         i = g - n_full
-        remote(l_all.at[i], l_all.at[i], sent, l_recv.at[1, i], sib).wait_recv()
+        remote(l_all.at[i], l_all.at[i], sent, (q_recv.at[4], c_recv.at[0])[i], sib).wait_recv()
         put(2 * groups[g][0] // 8, rows_of(g), l_sum[i] + l_all[i, 0], l_all[i, 2] + l_all[i, 1])
 
     def join(g, rows, mine, other):
@@ -366,7 +367,7 @@
     for g in range(n_full):
         y_final(g)
     half_final(3)
-    remote(f_rcv, f_rcv, sent, f_recv, sib).wait_recv()
+    remote(f_rcv, f_rcv, sent, a_recv.at[2], sib).wait_recv()
     for g in range(n_full):
         join(g, slice(None), f_src[g], f_rcv[g])
     half_copy().wait_recv()
@@ -375,10 +376,10 @@
     remote(qall.at[0:3], qall.at[0:3], sent, q_recv.at[0], sib).wait_send()
     remote(r1, r1, sent, a_recv.at[0], sib).wait_send()
     remote(r2, r2, sent, c_recv.at[0], cnt).wait_send()
-    remote(f_rcv, f_rcv, sent, f_recv, sib).wait_send()
-    remote(y_src, y_src, sent, y_recv.at[0, 0], sib).wait_send()
-    remote(l_r1, l_r1, sent, l_recv.at[0, 0], sib).wait_send()
-    remote(l_src, l_src, sent, l_recv.at[0, 0], sib).wait_send()
+    remote(f_rcv, f_rcv, sent, a_recv.at[2], sib).wait_send()
+    remote(y_src, y_src, sent, q_recv.at[0], sib).wait_send()
+    remote(l_r1, l_r1, sent, a_recv.at[0], sib).wait_send()
+    remote(l_src, l_src, sent, a_recv.at[0], sib).wait_send()
     last_final(4)
 
 
@@ -455,10 +456,6 @@
                 dma((7,)),
                 dma((10,)),
                 dma((5,)),
-                dma((2, 3)),
-                dma(()),
-                dma(()),
-                dma((2, 2)),
             ],
             compiler_params=pltpu.CompilerParams(
                 collective_id=0, has_side_effects=True, vmem_limit_bytes=53 * 1024 * 1024,

time: 33.8 us -> 33.7 us (level)
  no operation moved by 1% of the time
where the time goes in v8:
time: 33.7 us; the launch traced here: 33.6 us
  Pallas kernels  32.9 us (98%)
  local copies, waits for them, and re-layouts  0.66 us (2%)
    pallas_call x1, Pallas kernels, mla_step(): pl.pallas_call(kernel, out_shape=jax.ShapeDtypeStruct((n_group, 8, d_mode...  32.9 us

profile of v8, /device:TPU:0, one launch (start us, length us, event | category | flops | bytes accessed | tf_op | source)
XLA Modules:
  0.0 33.6 jit_solution(4488333961641203928)
XLA Ops:
  0.0 32.9 %mla_decode.1 = bf16[4,8,2048]{2,1,0:T(8,128)(2,1)S(1)} custom-call(s32[32]{0:T(128)} %len_hbm.1, bf16[32,2048]{1,0:T(8,128)(2,1)} %hid_hbm.1, bf16[4,8,2048]{2,1,0:T(8,128)(2,1)} %bitcast.15, bf16[8192,128]{1,0:T(8,128)(2,1)} %bitcast.11, bf16[256,2048]{1,0:T(8,128)(2,1)} %bitcast.13, bf16[512,512]{1,0:T(8,128)(2,1)} %bitcast.14, ...), custom_call_target="tpu_custom_call" | custom-call | tf_op jit(solution)/shard_map/mla_decode/pallas_call | solution.py:416
  32.9 0.7 %copy.11 = bf16[32,2048]{1,0:T(8,128)(2,1)} copy(bf16[32,2048]{1,0:T(8,128)(2,1)S(1)} %bitcast.9) | data formatting | bytes 262144

commit v9 on v8

--- a/solution.py
+++ b/solution.py
@@ -120,7 +120,8 @@
 
     def q_copy(kind, g):
         forward = g >= n_direct and kind == 1
-        slot, peer = ((me, cnt), (cnt, sib) if forward else (me, far), (me, sib))[kind]
+        first = cnt if g >= n_direct else 2 * (1 - x)
+        slot, peer = ((me, first), (cnt, sib) if forward else (me, 2 * (1 - x) + 1), (me, sib))[kind]
         rows = qall.at[slot, chunks[g][0]:chunks[g][1]]
         return remote(rows, rows, sent, q_recv.at[g + 2 if g >= n_direct and kind == 0 else g], peer)
 
@@ -178,7 +179,8 @@
 
     def pair_copy(ps):
         rows = slice(2 * ps[0], 2 * ps[-1] + 2)
-        return remote(acc_src.at[1 - c, rows], r1.at[rows], sent, a_recv.at[sends.index(ps)], sib)
+        i = sends.index(ps)
+        return remote(acc_src.at[1 - c, rows], r1.at[rows], sent, a_recv.at[i] if i < 6 else ckv_sem.at[i - 6], sib)
 
     def chip_copy(ps):
         rows = slice(ps[0], ps[-1] + 1)
@@ -454,7 +456,7 @@
                 dma((5,)),
                 dma(()),
                 dma((7,)),
-                dma((10,)),
+                dma((6,)),
                 dma((5,)),
             ],
             compiler_params=pltpu.CompilerParams(

time: 33.7 us -> 33.5 us (level)
  no operation moved by 1% of the time
where the time goes in v9:
time: 33.5 us; the launch traced here: 33.4 us
  Pallas kernels  32.7 us (98%)
  local copies, waits for them, and re-layouts  0.66 us (2%)
    pallas_call x1, Pallas kernels, mla_step(): pl.pallas_call(kernel, out_shape=jax.ShapeDtypeStruct((n_group, 8, d_mode...  32.7 us

profile of v9, /device:TPU:0, one launch (start us, length us, event | category | flops | bytes accessed | tf_op | source)
XLA Modules:
  0.0 33.4 jit_solution(15314791837218883261)
XLA Ops:
  0.0 32.7 %mla_decode.1 = bf16[4,8,2048]{2,1,0:T(8,128)(2,1)S(1)} custom-call(s32[32]{0:T(128)} %len_hbm.1, bf16[32,2048]{1,0:T(8,128)(2,1)} %hid_hbm.1, bf16[4,8,2048]{2,1,0:T(8,128)(2,1)} %bitcast.15, bf16[8192,128]{1,0:T(8,128)(2,1)} %bitcast.11, bf16[256,2048]{1,0:T(8,128)(2,1)} %bitcast.13, bf16[512,512]{1,0:T(8,128)(2,1)} %bitcast.14, ...), custom_call_target="tpu_custom_call" | custom-call | tf_op jit(solution)/shard_map/mla_decode/pallas_call | solution.py:418
  32.7 0.7 %copy.11 = bf16[32,2048]{1,0:T(8,128)(2,1)} copy(bf16[32,2048]{1,0:T(8,128)(2,1)S(1)} %bitcast.9) | data formatting | bytes 262144
